TPU v7x, 16 devices: a 4x2x1 block of a 4x4x8 slice. The times are simulated.
16 devices in a mesh: replica: 2 (over y, z), data: 8 (over x, core).
Axes of the slice: x: 4, y: 2, z: 1, core: 2. Of those that a mesh axis runs over, the one named last changes fastest.
The devices are a block of a 4x4x8 slice.
Arguments:
- x: bfloat16 [16384, 2048], P(('replica', 'data')), parts along dimension 0
- adapter_id: int32 [16384], P(('replica', 'data')), parts along dimension 0
- w_gate: bfloat16 [2048, 5632], replicated
- w_up: bfloat16 [2048, 5632], replicated
- w_down: bfloat16 [5632, 2048], replicated
- a_gate: bfloat16 [32, 2048, 64], P('data')
- b_gate: bfloat16 [32, 64, 5632], P('data')
- a_up: bfloat16 [32, 2048, 64], P('data')
- b_up: bfloat16 [32, 64, 5632], P('data')
- a_down: bfloat16 [32, 5632, 64], P('data')
- b_down: bfloat16 [32, 64, 2048], P('data')
- hot_ids: int32 [4], replicated
- hot_a_gate: bfloat16 [4, 2048, 64], replicated
- hot_b_gate: bfloat16 [4, 64, 5632], replicated
- hot_a_up: bfloat16 [4, 2048, 64], replicated
- hot_b_up: bfloat16 [4, 64, 5632], replicated
- hot_a_down: bfloat16 [4, 5632, 64], replicated
- hot_b_down: bfloat16 [4, 64, 2048], replicated
Outputs:
- output: bfloat16 [16384, 2048], P(('replica', 'data')), parts along dimension 0
There are 2 independent parts. A program takes and returns all parts, laid end to end along the dimension named above; an argument that names none is the same for every part.
All inputs are finite; a program needn't handle non-finite values.
Results may differ from a plain program's by a relative error of at most 0.00179.
Values are sent between devices in bfloat16 or wider.
A program may use at most 768 MiB of HBM per device.

v0:
```python
import jax
import jax.numpy as jnp
from jax import lax
from jax.sharding import PartitionSpec as P

value_a10 = 32


def route_layout(tok_ids, hot_ids, group_size, n_local, capacity):
    tok_count = tok_ids.shape[0]
    hot_match = tok_ids[:, None] == hot_ids[None, :]
    is_hot = jnp.any(hot_match, axis=1)
    owner_of = jnp.where(is_hot, group_size, tok_ids // n_local)
    sort_order = jnp.argsort(owner_of, stable=True)
    counts = jax.ops.segment_sum(jnp.ones_like(owner_of), owner_of, num_segments=group_size + 1)
    starts = jnp.cumsum(counts) - counts
    within = jnp.arange(capacity)
    slot_tok = sort_order[jnp.minimum(starts[:group_size, None] + within[None, :], tok_count - 1)].reshape(-1)
    slot_ok = (within[None, :] < counts[:group_size, None]).reshape(-1)
    sort_rank = jnp.zeros_like(owner_of).at[sort_order].set(jnp.arange(tok_count, dtype=owner_of.dtype))
    owner_safe = jnp.minimum(owner_of, group_size - 1)
    tok_slot = owner_safe * capacity + jnp.clip(sort_rank - starts[owner_safe], 0, capacity - 1)
    return hot_match.astype(jnp.bfloat16), is_hot, slot_tok, slot_ok, tok_slot


def adapter_delta(tok_rows, select, a_set, b_set, array_b10):
    low_rank = jnp.einsum("md,ndr->mnr", tok_rows, a_set, preferred_element_type=jnp.float32).astype(jnp.bfloat16)
    low_rank = low_rank * select[:, :, None]
    delta_f = jnp.einsum("mnr,nrf->mf", low_rank, b_set, preferred_element_type=jnp.float32)
    return (array_b10 * delta_f).astype(jnp.bfloat16)


def solution(mesh):
    group_size = mesh.shape["data"]
    token_spec = P(("replica", "data"), None)
    store_spec = P("data", None, None)
    full_mat = P(None, None)
    full_set = P(None, None, None)
    in_specs = (token_spec, P(("replica", "data")), full_mat, full_mat, full_mat) + (store_spec,) * 6 + (P(None),) + (full_set,) * 6

    def device_step(x, adapter_id, w_gate, w_up, w_down, a_gate, b_gate, a_up, b_up, a_down, b_down, hot_ids, hot_a_gate, hot_b_gate, hot_a_up, hot_b_up, hot_a_down, hot_b_down):
        tok_count = x.shape[0]
        n_local = a_gate.shape[0]
        array_b10 = value_a10 / a_gate.shape[2]
        capacity = tok_count // (2 * group_size)
        hot_sel, is_hot, slot_tok, slot_ok, tok_slot = route_layout(adapter_id, hot_ids, group_size, n_local, capacity)

        def exchange(send_rows):
            return lax.all_to_all(send_rows, "data", 0, 0, tiled=True)

        def to_tokens(back_rows):
            return jnp.where(is_hot[:, None], 0.0, jnp.take(back_rows, tok_slot, axis=0).astype(jnp.float32))

        send_ids = jnp.where(slot_ok, jnp.take(adapter_id, slot_tok), -1)
        recv_ids = exchange(send_ids) - lax.axis_index("data") * n_local
        owner_sel = (recv_ids[:, None] == jnp.arange(n_local)[None, :]).astype(jnp.bfloat16)

        recv_x = exchange(jnp.take(x, slot_tok, axis=0))
        gate_back = exchange(adapter_delta(recv_x, owner_sel, a_gate, b_gate, array_b10))
        up_back = exchange(adapter_delta(recv_x, owner_sel, a_up, b_up, array_b10))
        gate_act = (jnp.dot(x, w_gate, preferred_element_type=jnp.float32)
                    + adapter_delta(x, hot_sel, hot_a_gate, hot_b_gate, array_b10).astype(jnp.float32)
                    + to_tokens(gate_back))
        up_act = (jnp.dot(x, w_up, preferred_element_type=jnp.float32)
                  + adapter_delta(x, hot_sel, hot_a_up, hot_b_up, array_b10).astype(jnp.float32)
                  + to_tokens(up_back))
        hidden = (jax.nn.silu(gate_act) * up_act).astype(jnp.bfloat16)

        recv_h = exchange(jnp.take(hidden, slot_tok, axis=0))
        down_back = exchange(adapter_delta(recv_h, owner_sel, a_down, b_down, array_b10))
        down_out = (jnp.dot(hidden, w_down, preferred_element_type=jnp.float32)
                    + adapter_delta(hidden, hot_sel, hot_a_down, hot_b_down, array_b10).astype(jnp.float32)
                    + to_tokens(down_back))
        return (x.astype(jnp.float32) + down_out).astype(jnp.bfloat16)

    return jax.shard_map(device_step, mesh=mesh, in_specs=in_specs, out_specs=token_spec, check_vma=False)
```

profile of v0, /device:TPU:113, one launch (start us, length us, event | category | flops | bytes accessed | tf_op | source)
XLA Modules:
  0.0 455.2 jit_solution(11853696814011446597)
XLA Ops:
  1.7 7.6 %scatter_custom_fusion = s32[9]{0:T(128)S(1)} fusion(s32[1024]{0:T(1024)S(1)} %fusion.26, s32[1024]{0:T(1024)S(1)} %ne.14, s32[]{:T(128)} %constant.67.clone.1), kind=kCustom, calls=%fused_computation.78 | custom fusion | flops 1024 | bytes 40 | tf_op jit(solution)/shard_map/scatter-add | solution.py:15
  9.6 4.4 sort.17
  16.4 3.4 gather_fusion.2
  20.5 6.0 %all-to-all-start.1 = ((s32[8,64,1]{1,2,0:T(1,128)}), s32[8,64,1]{1,2,0:T(1,128)S(1)}, u32[]{:S(2)}, u32[]{:S(2)}) async-start(s32[8,64,1]{1,2,0:T(1,128)} %bitcast.22), calls=%async_computation.1 | async-start | bytes 8192 | tf_op jit(solution)/shard_map/all_to_all | solution.py:49
  26.6 8.0 %gather_fusion.1 = bf16[512,2048]{1,0:T(8,128)(2,1)} fusion(bf16[1024,2048]{1,0:T(8,128)(2,1)} %param.20, s32[1024]{0:T(1024)S(1)} %pad_clamp_fusion), kind=kCustom, calls=%fused_computation.3 | custom fusion | bytes 4196352 | tf_op jit(solution)/shard_map/jit(_take)/gather | solution.py:58
  34.6 3.2 broadcast_select_fusion.1
  37.7 4.8 %all-to-all-start = ((bf16[8,64,2048]{2,1,0:T(8,128)(2,1)}), bf16[8,64,2048]{2,1,0:T(8,128)(2,1)}, u32[]{:S(2)}, u32[]{:S(2)}) async-start(bf16[8,64,2048]{2,1,0:T(8,128)(2,1)} %broadcast_select_fusion.1), calls=%async_computation | async-start | bytes 4194304 | tf_op jit(solution)/shard_map/all_to_all | solution.py:49
  42.5 4.3 scatter_custom_fusion.1
  47.6 21.0 %all-to-all-done = bf16[8,64,2048]{2,1,0:T(8,128)(2,1)} async-done(((bf16[8,64,2048]{2,1,0:T(8,128)(2,1)}), bf16[8,64,2048]{2,1,0:T(8,128)(2,1)}, u32[]{:S(2)}, u32[]{:S(2)}) %all-to-all-start) | async-done | bytes 2097184 | tf_op jit(solution)/shard_map/all_to_all | solution.py:49
  71.2 5.9 %fusion.3 = bf16[512,5632]{1,0:T(8,128)(2,1)} fusion(bf16[4,64,5632]{2,1,0:T(8,128)(2,1)} %param.26, f32[512,4,64]{0,2,1:T(8,128)S(1)} %bitcast.125, bf16[512,4]{0,1:T(4,128)(2,1)S(1)} %fusion.24), kind=kOutput, calls=%fused_computation.17 | convolution fusion | flops 1482424320 | bytes 9179136 | tf_op jit(solution)/shard_map/mnr,nrf->mf/dot_general | solution.py:29
  77.2 6.3 %all-to-all-start.2 = ((bf16[8,64,5632]{2,1,0:T(8,128)(2,1)}), bf16[8,64,5632]{2,1,0:T(8,128)(2,1)}, u32[]{:S(2)}, u32[]{:S(2)}) async-start(bf16[8,64,5632]{2,1,0:T(8,128)(2,1)} %bitcast.105), calls=%async_computation.2 | async-start | bytes 11534336 | tf_op jit(solution)/shard_map/all_to_all | solution.py:49
  83.6 6.2 %compare_and_fusion = (pred[1024]{0:T(1024)(128)(4,1)S(1)}, s32[1024]{0:T(1024)S(1)}) fusion(s32[1024]{0:T(1024)S(1)} %scatter_custom_fusion.1, s32[]{:T(128)} %bitcast.14, s32[]{:T(128)} %bitcast.13, s32[]{:T(128)} %bitcast.12, s32[]{:T(128)} %bitcast.11, s32[]{:T(128)} %bitcast.10, s32[]{:T(128)} %bitcast.9, s32[]{:T(128)} %bitcast.8, s32[]{:T(128)} %bitcast.7, ...), kind=kLoop, calls=%fused_computation.70 | loop fusion | flops 30720 | bytes 13348 | tf_op jit(solution)/shard_map/jit(_take)/and | solution.py:52
  89.8 3.8 fusion.38
  94.9 6.1 %fusion = bf16[1024,5632]{1,0:T(8,128)(2,1)} fusion(bf16[4,64,5632]{2,1,0:T(8,128)(2,1)S(1)} %copy-done, f32[1024,4,64]{0,2,1:T(8,128)S(1)} %bitcast.121, bf16[1024,4]{0,1:T(4,128)(2,1)S(1)} %get-tuple-element.11), kind=kOutput, calls=%fused_computation.10 | convolution fusion | flops 2964848640 | bytes 15474688 | tf_op jit(solution)/shard_map/mnr,nrf->mf/dot_general | solution.py:29
  100.9 6.1 %fusion.1 = bf16[1024,5632]{1,0:T(8,128)(2,1)} fusion(bf16[4,64,5632]{2,1,0:T(8,128)(2,1)S(1)} %copy-done.13, f32[1024,4,64]{0,2,1:T(8,128)S(1)} %bitcast.120, bf16[1024,4]{0,1:T(4,128)(2,1)S(1)} %get-tuple-element.11), kind=kOutput, calls=%fused_computation.12 | convolution fusion | flops 2964848640 | bytes 15474688 | tf_op jit(solution)/shard_map/mnr,nrf->mf/dot_general | solution.py:29
  109.6 4.1 fusion.2
  113.7 35.2 %all-to-all-done.2 = bf16[8,64,5632]{2,1,0:T(8,128)(2,1)} async-done(((bf16[8,64,5632]{2,1,0:T(8,128)(2,1)}), bf16[8,64,5632]{2,1,0:T(8,128)(2,1)}, u32[]{:S(2)}, u32[]{:S(2)}) %all-to-all-start.2) | async-done | bytes 5767200 | tf_op jit(solution)/shard_map/all_to_all | solution.py:49
  148.9 6.0 %all-to-all-start.3 = ((bf16[8,64,5632]{2,1,0:T(8,128)(2,1)}), bf16[8,64,5632]{2,1,0:T(8,128)(2,1)}, u32[]{:S(2)}, u32[]{:S(2)}) async-start(bf16[8,64,5632]{2,1,0:T(8,128)(2,1)} %bitcast.106), calls=%async_computation.3 | async-start | bytes 11534336 | tf_op jit(solution)/shard_map/all_to_all | solution.py:49
  154.9 33.9 %fusion.37 = f32[1024,5632]{1,0:T(8,128)} fusion(bf16[1024,2048]{1,0:T(8,128)(2,1)} %param.20, bf16[2048,5632]{1,0:T(8,128)(2,1)} %param.22), kind=kOutput, calls=%fused_computation.81 | convolution fusion | flops 23622320128 | bytes 50331648 | tf_op jit(solution)/shard_map/dot_general | solution.py:61
  188.8 23.6 %gather_fusion.5 = bf16[1024,5632]{1,0:T(8,128)(2,1)} fusion(bf16[512,5632]{1,0:T(8,128)(2,1)} %bitcast.25, s32[1024]{0:T(1024)S(1)} %broadcast_clamp_fusion), kind=kCustom, calls=%fused_computation.clone | custom fusion | bytes 23072768 | tf_op jit(solution)/shard_map/jit(_take)/gather | solution.py:52
  212.4 7.9 %all-to-all-done.3 = bf16[8,64,5632]{2,1,0:T(8,128)(2,1)} async-done(((bf16[8,64,5632]{2,1,0:T(8,128)(2,1)}), bf16[8,64,5632]{2,1,0:T(8,128)(2,1)}, u32[]{:S(2)}, u32[]{:S(2)}) %all-to-all-start.3) | async-done | bytes 5767200 | tf_op jit(solution)/shard_map/all_to_all | solution.py:49
  220.3 23.4 %gather_fusion.6 = bf16[1024,5632]{1,0:T(8,128)(2,1)} fusion(bf16[512,5632]{1,0:T(8,128)(2,1)} %bitcast.35, s32[1024]{0:T(1024)S(1)} %broadcast_clamp_fusion), kind=kCustom, calls=%fused_computation.1.clone | custom fusion | bytes 23072768 | tf_op jit(solution)/shard_map/jit(_take)/gather | solution.py:52
  243.7 46.2 %multiply_convert_fusion = bf16[1024,5632]{1,0:T(8,128)(2,1)} fusion(bf16[1024,5632]{1,0:T(8,128)(2,1)} %fusion, f32[1024,5632]{1,0:T(8,128)} %fusion.37, bf16[1024,5632]{1,0:T(8,128)(2,1)} %fusion.1, bf16[1024,2048]{1,0:T(8,128)(2,1)} %param.20, bf16[2048,5632]{1,0:T(8,128)(2,1)} %param.23, bf16[1024,5632]{1,0:T(8,128)(2,1)} %gather_fusion.6, ...), kind=kOutput, calls=%fused_computation.13 | convolution fusion | flops 23726129152 | bytes 108005376 | tf_op jit(solution)/shard_map/dot_general | solution.py:64
  289.9 17.3 %gather_fusion.3 = bf16[512,5632]{1,0:T(8,128)(2,1)} fusion(bf16[1024,5632]{1,0:T(8,128)(2,1)} %multiply_convert_fusion, s32[1024]{0:T(1024)S(1)} %copy-done.4), kind=kCustom, calls=%fused_computation.5 | custom fusion | bytes 11536384 | tf_op jit(solution)/shard_map/jit(_take)/gather | solution.py:69
  307.2 3.2 broadcast_select_fusion
  310.4 69.4 %all_to_all.60 = bf16[8,64,5632]{2,1,0:T(8,128)(2,1)S(1)} all-to-all(bf16[8,64,5632]{2,1,0:T(8,128)(2,1)S(1)} %broadcast_select_fusion), channel_id=1, replica_groups=mesh['replica'=2,'data'=8] {'data'}, dimensions={0} | all-to-all | bytes 11534336 | tf_op jit(solution)/shard_map/all_to_all | solution.py:49
  383.6 5.1 %all-to-all-start.5 = ((bf16[8,64,2048]{2,1,0:T(8,128)(2,1)}), bf16[8,64,2048]{2,1,0:T(8,128)(2,1)S(1)}, u32[]{:S(2)}, u32[]{:S(2)}) async-start(bf16[8,64,2048]{2,1,0:T(8,128)(2,1)} %bitcast.108), calls=%async_computation.5 | async-start | bytes 4194304 | tf_op jit(solution)/shard_map/all_to_all | solution.py:49
  388.7 7.0 %fusion.42 = f32[1024,256]{0,1:S(1)} fusion(bf16[1024,5632]{1,0:T(8,128)(2,1)} %multiply_convert_fusion, bf16[5632,256]{0,1:T(8,128)(2,1)} %bitcast.115), kind=kOutput, calls=%fused_computation.86 | convolution fusion | flops 2952790016 | bytes 15466496
  395.7 3.3 fusion.4
  399.1 15.6 %all-to-all-done.5 = bf16[8,64,2048]{2,1,0:T(8,128)(2,1)S(1)} async-done(((bf16[8,64,2048]{2,1,0:T(8,128)(2,1)}), bf16[8,64,2048]{2,1,0:T(8,128)(2,1)S(1)}, u32[]{:S(2)}, u32[]{:S(2)}) %all-to-all-start.5) | async-done | bytes 2097184 | tf_op jit(solution)/shard_map/all_to_all | solution.py:49
  414.7 6.0 %gather_fusion.4 = bf16[1024,2048]{1,0:T(8,128)(2,1)} fusion(bf16[512,2048]{1,0:T(8,128)(2,1)S(1)} %bitcast.102, s32[1024]{0:T(1024)S(1)} %broadcast_clamp_fusion), kind=kCustom, calls=%fused_computation.6 | custom fusion | bytes 8392704 | tf_op jit(solution)/shard_map/jit(_take)/gather | solution.py:52
  420.7 34.0 %add_convert_fusion = bf16[1024,2048]{1,0:T(8,128)(2,1)} fusion(bf16[1024,2048]{1,0:T(8,128)(2,1)} %fusion.4, bf16[1024,2048]{1,0:T(8,128)(2,1)} %param.20, bf16[1024,2048]{1,0:T(8,128)(2,1)} %gather_fusion.4, pred[1024]{0:T(1024)(128)(4,1)S(1)} %get-tuple-element.8, pred[1024]{0:T(1024)(128)(4,1)S(1)} %copy-done.10, ...), kind=kOutput, calls=%fused_computation.20 | convolution fusion | flops 23641194496 | bytes 51382272 | tf_op jit(solution)/shard_map/dot_general | solution.py:71
  (70 shorter events, 16.1 us)
Async XLA Ops:
  0.0 94.8 %copy-start = (bf16[4,64,5632]{2,1,0:T(8,128)(2,1)S(1)}, bf16[4,64,5632]{2,1,0:T(8,128)(2,1)}, u32[]{:S(2)}) copy-start(bf16[4,64,5632]{2,1,0:T(8,128)(2,1)} %param.35) | copy-start | bytes 8650756
  0.9 8.6 %copy-start.9 = (pred[1024]{0:T(1024)(128)(4,1)}, pred[1024]{0:T(1024)(128)(4,1)S(1)}, u32[]{:S(2)}) copy-start(pred[1024]{0:T(1024)(128)(4,1)S(1)} %get-tuple-element.10) | copy-start | bytes 3076
  0.9 100.0 %copy-start.7 = (bf16[1024,4]{0,1:T(4,128)(2,1)}, bf16[1024,4]{0,1:T(4,128)(2,1)S(1)}, u32[]{:S(2)}) copy-start(bf16[1024,4]{0,1:T(4,128)(2,1)S(1)} %get-tuple-element.11) | copy-start | bytes 24580
  16.4 18.2 %copy-start.3 = (s32[1024]{0:T(1024)}, s32[1024]{0:T(1024)S(1)}, u32[]{:S(2)}) copy-start(s32[1024]{0:T(1024)S(1)} %pad_clamp_fusion) | copy-start | bytes 12292
  20.5 17.2 %all-to-all-start.1 = ((s32[8,64,1]{1,2,0:T(1,128)}), s32[8,64,1]{1,2,0:T(1,128)S(1)}, u32[]{:S(2)}, u32[]{:S(2)}) async-start(s32[8,64,1]{1,2,0:T(1,128)} %bitcast.22), calls=%async_computation.1 | async-start | bytes 8192 | tf_op jit(solution)/shard_map/all_to_all | solution.py:49
  26.6 8.0 %copy-start.5 = (pred[8,64]{1,0:T(8,128)(4,1)}, pred[8,64]{1,0:T(8,128)(4,1)S(1)}, u32[]{:S(2)}) copy-start(pred[8,64]{1,0:T(8,128)(4,1)S(1)} %compare_and_fusion.1) | copy-start | bytes 1540
  37.7 30.9 %all-to-all-start = ((bf16[8,64,2048]{2,1,0:T(8,128)(2,1)}), bf16[8,64,2048]{2,1,0:T(8,128)(2,1)}, u32[]{:S(2)}, u32[]{:S(2)}) async-start(bf16[8,64,2048]{2,1,0:T(8,128)(2,1)} %broadcast_select_fusion.1), calls=%async_computation | async-start | bytes 4194304 | tf_op jit(solution)/shard_map/all_to_all | solution.py:49
  47.6 61.9 %copy-start.11 = (bf16[512,4]{0,1:T(4,128)(2,1)}, bf16[512,4]{0,1:T(4,128)(2,1)S(1)}, u32[]{:S(2)}) copy-start(bf16[512,4]{0,1:T(4,128)(2,1)S(1)} %fusion.24) | copy-start | bytes 12292
  77.2 71.7 %all-to-all-start.2 = ((bf16[8,64,5632]{2,1,0:T(8,128)(2,1)}), bf16[8,64,5632]{2,1,0:T(8,128)(2,1)}, u32[]{:S(2)}, u32[]{:S(2)}) async-start(bf16[8,64,5632]{2,1,0:T(8,128)(2,1)} %bitcast.105), calls=%async_computation.2 | async-start | bytes 11534336 | tf_op jit(solution)/shard_map/all_to_all | solution.py:49
  83.5 10.0 %copy-start.2 = (bf16[1024,2048]{1,0:T(8,128)(2,1)S(1)}, bf16[1024,2048]{1,0:T(8,128)(2,1)}, u32[]{:S(2)}) copy-start(bf16[1024,2048]{1,0:T(8,128)(2,1)} %param.20) | copy-start | bytes 12582916
  83.5 10.0 %copy-start.16 = (bf16[4,2048,64]{1,2,0:T(8,128)(2,1)S(1)}, bf16[4,2048,64]{1,2,0:T(8,128)(2,1)}, u32[]{:S(2)}) copy-start(bf16[4,2048,64]{1,2,0:T(8,128)(2,1)} %param.34) | copy-start | bytes 3145732
  94.8 6.1 %copy-start.13 = (bf16[4,64,5632]{2,1,0:T(8,128)(2,1)S(1)}, bf16[4,64,5632]{2,1,0:T(8,128)(2,1)}, u32[]{:S(2)}) copy-start(bf16[4,64,5632]{2,1,0:T(8,128)(2,1)} %param.33) | copy-start | bytes 8650756
  100.9 6.1 %copy-start.17 = (bf16[4,2048,64]{1,2,0:T(8,128)(2,1)S(1)}, bf16[4,2048,64]{1,2,0:T(8,128)(2,1)}, u32[]{:S(2)}) copy-start(bf16[4,2048,64]{1,2,0:T(8,128)(2,1)} %param.27) | copy-start | bytes 3145732
  100.9 8.6 %copy-start.14 = (bf16[4,64,5632]{2,1,0:T(8,128)(2,1)S(1)}, bf16[4,64,5632]{2,1,0:T(8,128)(2,1)}, u32[]{:S(2)}) copy-start(bf16[4,64,5632]{2,1,0:T(8,128)(2,1)} %param.28) | copy-start | bytes 8650756
  148.9 71.4 %all-to-all-start.3 = ((bf16[8,64,5632]{2,1,0:T(8,128)(2,1)}), bf16[8,64,5632]{2,1,0:T(8,128)(2,1)}, u32[]{:S(2)}, u32[]{:S(2)}) async-start(bf16[8,64,5632]{2,1,0:T(8,128)(2,1)} %bitcast.106), calls=%async_computation.3 | async-start | bytes 11534336 | tf_op jit(solution)/shard_map/all_to_all | solution.py:49
  220.3 23.4 %copy-start.10 = (pred[1024]{0:T(1024)(128)(4,1)S(1)}, pred[1024]{0:T(1024)(128)(4,1)}, u32[]{:S(2)}) copy-start(pred[1024]{0:T(1024)(128)(4,1)} %copy-done.9) | copy-start | bytes 3076
  243.7 46.2 %copy-start.4 = (s32[1024]{0:T(1024)S(1)}, s32[1024]{0:T(1024)}, u32[]{:S(2)}) copy-start(s32[1024]{0:T(1024)} %copy-done.3) | copy-start | bytes 12292
  289.9 17.3 %copy-start.6 = (pred[8,64]{1,0:T(8,128)(4,1)S(1)}, pred[8,64]{1,0:T(8,128)(4,1)}, u32[]{:S(2)}) copy-start(pred[8,64]{1,0:T(8,128)(4,1)} %copy-done.5) | copy-start | bytes 1540
  310.4 69.5 %copy-start.15 = (bf16[4,5632,64]{1,2,0:T(8,128)(2,1)S(1)}, bf16[4,5632,64]{1,2,0:T(8,128)(2,1)}, u32[]{:S(2)}) copy-start(bf16[4,5632,64]{1,2,0:T(8,128)(2,1)} %param.29) | copy-start | bytes 8650756
  379.8 1.7 copy-start.12
  379.8 1.7 copy-start.18
  383.6 31.1 %all-to-all-start.5 = ((bf16[8,64,2048]{2,1,0:T(8,128)(2,1)}), bf16[8,64,2048]{2,1,0:T(8,128)(2,1)S(1)}, u32[]{:S(2)}, u32[]{:S(2)}) async-start(bf16[8,64,2048]{2,1,0:T(8,128)(2,1)} %bitcast.108), calls=%async_computation.5 | async-start | bytes 4194304 | tf_op jit(solution)/shard_map/all_to_all | solution.py:49
  388.7 7.0 %copy-start.8 = (bf16[1024,4]{0,1:T(4,128)(2,1)S(1)}, bf16[1024,4]{0,1:T(4,128)(2,1)}, u32[]{:S(2)}) copy-start(bf16[1024,4]{0,1:T(4,128)(2,1)} %copy-done.7) | copy-start | bytes 24580
  388.7 7.0 %copy-start.19 = (bf16[4,64,2048]{2,1,0:T(8,128)(2,1)S(1)}, bf16[4,64,2048]{2,1,0:T(8,128)(2,1)}, u32[]{:S(2)}) copy-start(bf16[4,64,2048]{2,1,0:T(8,128)(2,1)} %param.37) | copy-start | bytes 3145732
  420.7 34.0 %copy-start.1 = (bf16[4,64,5632]{2,1,0:T(8,128)(2,1)S(1)}, bf16[4,64,5632]{2,1,0:T(8,128)(2,1)}, u32[]{:S(2)}) copy-start(bf16[4,64,5632]{2,1,0:T(8,128)(2,1)} %param.35) | copy-start | bytes 8650756
where the time goes:
time: 464 us; the launch traced here: 455 us
  matrix products  161 us (35%)
  local copies, waits for them, and re-layouts  89.3 us (19%)
  waiting for transfers between devices  79.7 us (17%)
  blocking collectives  69.4 us (15%)
  starting transfers between devices  28.3 us (6%)
  other arithmetic  27.1 us (6%)
    all_to_all x5, waiting for transfers between devices, exchange(): return lax.all_to_all(send_rows, 'data', 0, 0, tiled=True)  79.7 us
    all_to_all x1, blocking collectives, exchange(): return lax.all_to_all(send_rows, 'data', 0, 0, tiled=True)  69.4 us
    gather x3, local copies, waits for them, and re-layouts, to_tokens(): jnp.take(back_rows, tok_slot, axis=0).astype(jnp.float32)  52.9 us
    dot_general x1, matrix products, device_step(): jnp.dot(x, w_up, preferred_element_type=jnp.float32)  46.2 us
    dot_general x1, matrix products, device_step(): jnp.dot(hidden, w_down, preferred_element_type=jnp.float32)  34 us
    dot_general x1, matrix products, device_step(): jnp.dot(x, w_gate, preferred_element_type=jnp.float32)  33.9 us
    all_to_all x5, starting transfers between devices, exchange(): return lax.all_to_all(send_rows, 'data', 0, 0, tiled=True)  28.3 us
    dot_general x6, matrix products, adapter_delta(): jnp.einsum('mnr,nrf->mf', low_rank, b_set, preferred_element_type=jnp.flo...  27.7 us
  transfers between devices with their start and end apart: 5, of which 4 were waited for; matrix products, arithmetic and copies ran while one was open for 25% of the time, Pallas kernels for 0%

commit v1 on v0

v1 whole, which is shorter than its diff:
```python
import functools

import jax
import jax.numpy as jnp
from jax import lax
from jax.experimental import pallas as pl
from jax.experimental.pallas import tpu as pltpu
from jax.sharding import PartitionSpec as P

LORA_ALPHA = 32
BF16, F32, I32 = jnp.bfloat16, jnp.float32, jnp.int32
MESH = pl.DeviceIdType.MESH
GU_COLS = 512
SUB_COLS = 256
DN_COLS = 256


def nt_dot(rows, mat):
    return lax.dot_general(rows, mat, (((1,), (1,)), ((), ())), preferred_element_type=F32)


def nn_dot(rows, mat):
    return jnp.dot(rows, mat, preferred_element_type=F32)


def route(ids, hot_ids_ref, group, n_local, n_hot, cap):
    tok = ids.shape[1]
    hot = jnp.zeros(ids.shape, jnp.bool_)
    slot = jnp.zeros(ids.shape, I32)
    for j in range(n_hot):
        match = ids == hot_ids_ref[j]
        hot = hot | match
        slot = jnp.where(match, j, slot)
    owner = lax.div(ids, jnp.full(ids.shape, n_local, I32))
    slot = jnp.where(hot, slot, n_hot + ids - owner * n_local)
    key = jnp.where(hot, group, owner)
    n_rows = -(-(group + 1) // 16) * 16
    marks = (lax.broadcasted_iota(I32, (n_rows, tok), 0) == key).astype(F32)
    lane = 128
    before = (lax.broadcasted_iota(I32, (lane, lane), 0) < lax.broadcasted_iota(I32, (lane, lane), 1)).astype(F32).astype(BF16)
    total = jnp.zeros((n_rows, 1), F32)
    ranks = []
    for b in range(tok // lane):
        part = marks[:, b * lane:(b + 1) * lane]
        ranks.append(nn_dot(part.astype(BF16), before) + total)
        total = total + jnp.sum(part, axis=1, keepdims=True)
    rank = jnp.concatenate(ranks, axis=1)
    hot_rank = rank[group:group + 1, :]
    spare = jnp.zeros((1, 1), F32)
    place = jnp.zeros(ids.shape, F32)
    placed = jnp.zeros(ids.shape, F32)
    for j in range(group):
        count = total[j:j + 1, :]
        room = cap - count
        cold_place = rank[j:j + 1, :] + float(j * cap)
        place = jnp.where(key == j, cold_place, place)
        fits = (key == group) & (hot_rank >= spare) & (hot_rank < spare + room)
        place = jnp.where(fits, hot_rank - spare + (count + float(j * cap)), place)
        placed = jnp.where(fits, 1.0, placed)
        spare = spare + room
    kept = (key == group) & (placed == 0.0)
    place = jnp.where(kept, hot_rank - spare + float(group * cap), place)
    return place, slot.astype(F32)


def main_kernel(cfg, ids_ref, hot_ref, x_ref, wg_ref, wu_ref, wd_ref, ag_ref, bg_ref, au_ref, bu_ref, ad_ref, bd_ref,
                hag_ref, hbg_ref, hau_ref, hbu_ref, had_ref, hbd_ref,
                place_ref, back_ref, kept_ref,
                xs, meta, recv, recv_meta, h_kept, h_recv, at_g, at_u, at_d, b_d, wg, wu, bg, bu, wd, low_g, low_u, low_d,
                x_sem, w_sem, d_sem, a_sem, out_sem, send_sem, got_sem, msend_sem, mgot_sem, bsend_sem, bgot_sem):
    group, cap, n_local, n_hot, rank_dim, scale = cfg
    tok, dim = x_ref.shape
    hidden = wg_ref.shape[1]
    half = tok // 2
    hot_w, store_w = n_hot * rank_dim, n_local * rank_dim
    gu_tiles, dn_tiles = hidden // GU_COLS, dim // DN_COLS
    me = lax.axis_index("data")

    barrier = pltpu.get_barrier_semaphore()
    for k in range(1, group):
        pl.semaphore_signal(barrier, inc=1, device_id={"data": lax.rem(me + k, group)}, device_id_type=MESH)

    x_copies = [pltpu.make_async_copy(x_ref.at[pl.ds(i * half, half), :], h_recv.at[:, pl.ds(i * dim, dim)], x_sem.at[i]) for i in range(2)]
    for c in x_copies:
        c.start()
    adapters = [
        pltpu.make_async_copy(hag_ref, at_g.at[pl.ds(0, hot_w), :], a_sem.at[0]),
        pltpu.make_async_copy(hau_ref, at_u.at[pl.ds(0, hot_w), :], a_sem.at[1]),
        pltpu.make_async_copy(ag_ref, at_g.at[pl.ds(hot_w, store_w), :], a_sem.at[2]),
        pltpu.make_async_copy(au_ref, at_u.at[pl.ds(hot_w, store_w), :], a_sem.at[3]),
        pltpu.make_async_copy(had_ref, at_d.at[pl.ds(0, hot_w), :], a_sem.at[4]),
        pltpu.make_async_copy(ad_ref, at_d.at[pl.ds(hot_w, store_w), :], a_sem.at[5]),
        pltpu.make_async_copy(hbd_ref, b_d.at[pl.ds(0, hot_w), :], a_sem.at[6]),
        pltpu.make_async_copy(bd_ref, b_d.at[pl.ds(hot_w, store_w), :], a_sem.at[7]),
    ]

    def gu_copies(step):
        cols = pl.ds(pl.multiple_of(lax.rem(step, gu_tiles) * GU_COLS, GU_COLS), GU_COLS)
        s = lax.rem(step, 2)
        return [
            pltpu.make_async_copy(wg_ref.at[:, cols], wg.at[s], w_sem.at[s, 0]),
            pltpu.make_async_copy(wu_ref.at[:, cols], wu.at[s], w_sem.at[s, 1]),
            pltpu.make_async_copy(hbg_ref.at[:, cols], bg.at[s, pl.ds(0, hot_w), :], w_sem.at[s, 2]),
            pltpu.make_async_copy(hbu_ref.at[:, cols], bu.at[s, pl.ds(0, hot_w), :], w_sem.at[s, 3]),
            pltpu.make_async_copy(bg_ref.at[:, cols], bg.at[s, pl.ds(hot_w, store_w), :], w_sem.at[s, 4]),
            pltpu.make_async_copy(bu_ref.at[:, cols], bu.at[s, pl.ds(hot_w, store_w), :], w_sem.at[s, 5]),
        ]

    def dn_copy(step):
        cols = pl.ds(pl.multiple_of(lax.rem(step, dn_tiles) * DN_COLS, DN_COLS), DN_COLS)
        s = lax.rem(step, 2)
        return pltpu.make_async_copy(wd_ref.at[:, cols], wd.at[s], d_sem.at[s])

    for c in adapters[:2]:
        c.start()
    for c in gu_copies(jnp.int32(0)):
        c.start()
    for c in adapters[2:]:
        c.start()
    dn_copy(jnp.int32(0)).start()

    place, slot = route(ids_ref[...], hot_ref, group, n_local, n_hot, float(cap))
    place_i = place.astype(I32)
    slot_b = jnp.broadcast_to(slot, (128, tok)).astype(BF16)
    for c in x_copies:
        c.wait()

    def sort_rows(first, count):
        sel = (lax.broadcasted_iota(I32, (count, tok), 0) + first == place_i).astype(F32).astype(BF16)
        meta[pl.ds(first, count), :] = nt_dot(sel, slot_b).astype(BF16)
        for n in range(0, dim, 512):
            rows = nn_dot(sel[:, :half], h_recv[:, n:n + 512]) + nn_dot(sel[:, half:], h_recv[:, dim + n:dim + n + 512])
            xs[pl.ds(first, count), n:n + 512] = rows.astype(BF16)

    sort_rows(0, 256)
    sort_rows(256, 256)

    pl.semaphore_wait(barrier, group - 1)

    def x_copy(k):
        peer = lax.rem(me + k, group)
        src, dst = pl.ds(pl.multiple_of(peer * cap, cap), cap), pl.ds(pl.multiple_of(me * cap, cap), cap)
        return (
            pltpu.make_async_remote_copy(xs.at[src, :], recv.at[dst, :], send_sem.at[k - 1], got_sem.at[k - 1], device_id={"data": peer}, device_id_type=MESH),
            pltpu.make_async_remote_copy(meta.at[src, :], recv_meta.at[dst, :], msend_sem.at[k - 1], mgot_sem.at[k - 1], device_id={"data": peer}, device_id_type=MESH),
        )

    for k in range(1, group):
        for c in x_copy(k):
            c.start()

    sort_rows(512, 256)
    sort_rows(768, 256)
    place_ref[...] = jnp.transpose(jnp.broadcast_to(place, (128, tok))).astype(I32)
    mine = pl.ds(pl.multiple_of(me * cap, cap), cap)
    recv[mine, :] = xs[mine, :]
    recv_meta[mine, :] = meta[mine, :]

    def keep(low, slots, width):
        cols = jnp.concatenate([slots.astype(F32)] * (width // 128), axis=1)
        lanes = lax.div(lax.broadcasted_iota(I32, cols.shape, 1), jnp.full(cols.shape, rank_dim, I32)).astype(F32)
        return jnp.where(cols == lanes, low, 0.0).astype(BF16)

    def delta(low, mat):
        return (scale * nn_dot(low, mat)).astype(BF16).astype(F32)

    def gate_up(rows_ref, rows, slots, width, h_ref, first_step):
        low_g[:, :width] = keep(nt_dot(rows_ref[rows, :], at_g[:width, :]), slots, width)
        low_u[:, :width] = keep(nt_dot(rows_ref[rows, :], at_u[:width, :]), slots, width)

        @pl.loop(0, gu_tiles)
        def _(i):
            step = i + first_step
            for c in gu_copies(step):
                c.wait()

            @pl.when(step + 1 < 2 * gu_tiles)
            def _():
                for c in gu_copies(step + 1):
                    c.start()

            s = lax.rem(step, 2)
            for n in range(0, GU_COLS, SUB_COLS):
                sub = slice(n, n + SUB_COLS)
                g = nn_dot(rows_ref[rows, :], wg[s, :, sub]) + delta(low_g[:, :width], bg[s, :width, sub])
                u = nn_dot(rows_ref[rows, :], wu[s, :, sub]) + delta(low_u[:, :width], bu[s, :width, sub])
                h_ref[:, pl.ds(pl.multiple_of(i * GU_COLS + n, SUB_COLS), SUB_COLS)] = (jax.nn.silu(g) * u).astype(BF16)

    for c in adapters[:2]:
        c.wait()
    kept_rows = slice(half, tok)
    gate_up(xs, kept_rows, meta[kept_rows, :], hot_w, h_kept, 0)

    for c in adapters[2:]:
        c.wait()
    for k in range(1, group):
        for c in x_copy(k):
            c.wait_recv()
    gate_up(recv, slice(0, half), recv_meta[...], hot_w + store_w, h_recv, gu_tiles)

    def back_copy(p, k):
        peer = lax.rem(me + k, group)
        cols = pl.ds(pl.multiple_of(p * (2 * DN_COLS), 2 * DN_COLS), 2 * DN_COLS)
        return pltpu.make_async_remote_copy(
            recv.at[pl.ds(pl.multiple_of(peer * cap, cap), cap), cols], back_ref.at[pl.ds(pl.multiple_of(me * cap, cap), cap), cols],
            bsend_sem.at[p, k - 1], bgot_sem.at[p, k - 1], device_id={"data": peer}, device_id_type=MESH)

    def down(h_ref, rows_ref, rows, slots, width, first_step, after):
        low_d[:, :width] = keep(nt_dot(h_ref[...], at_d[:width, :]), slots, width)

        @pl.loop(0, dn_tiles // 2)
        def _(p):
            for q in range(2):
                i = p * 2 + q
                step = i + first_step
                dn_copy(step).wait()

                @pl.when(step + 1 < 2 * dn_tiles)
                def _():
                    dn_copy(step + 1).start()

                cols = pl.ds(pl.multiple_of(i * DN_COLS, DN_COLS), DN_COLS)
                y = nn_dot(h_ref[...], wd[lax.rem(step, 2)]) + delta(low_d[:, :width], b_d[:width, cols])
                rows_ref[rows, cols] = (rows_ref[rows, cols].astype(F32) + y).astype(BF16)
            after(p)

    def send_back(p):
        for k in range(1, group):
            back_copy(p, k).start()

    down(h_recv, recv, slice(0, half), recv_meta[...], hot_w + store_w, 0, send_back)
    own = pltpu.make_async_copy(recv.at[mine, :], back_ref.at[mine, :], out_sem.at[0])
    own.start()
    down(h_kept, xs, kept_rows, meta[kept_rows, :], hot_w, dn_tiles, lambda p: None)
    kept_out = pltpu.make_async_copy(xs.at[pl.ds(half, half), :], kept_ref, out_sem.at[1])
    kept_out.start()
    own.wait()
    kept_out.wait()
    for k in range(1, group):
        for c in x_copy(k):
            c.wait_send()

    @pl.loop(0, dn_tiles // 2)
    def _(p):
        for k in range(1, group):
            back_copy(p, k).wait()


def unsort_kernel(place_ref, back_ref, kept_ref, out_ref):
    count, half = out_ref.shape[0], back_ref.shape[0]
    dim = out_ref.shape[1]
    place = jnp.concatenate([place_ref[...]] * (2 * half // 128), axis=1)
    sel = (place == lax.broadcasted_iota(I32, (count, 2 * half), 1)).astype(F32).astype(BF16)
    for n in range(0, dim, 512):
        rows = nn_dot(sel[:, :half], back_ref[:, n:n + 512]) + nn_dot(sel[:, half:], kept_ref[:, n:n + 512])
        out_ref[:, n:n + 512] = rows.astype(BF16)


def solution(mesh):
    group = mesh.shape["data"]
    token_spec = P(("replica", "data"), None)
    store_spec = P("data", None, None)
    full_mat = P(None, None)
    full_set = P(None, None, None)
    in_specs = (token_spec, P(("replica", "data")), full_mat, full_mat, full_mat) + (store_spec,) * 6 + (P(None),) + (full_set,) * 6

    def device_step(x, adapter_id, w_gate, w_up, w_down, a_gate, b_gate, a_up, b_up, a_down, b_down, hot_ids, hot_a_gate, hot_b_gate, hot_a_up, hot_b_up, hot_a_down, hot_b_down):
        tok, dim = x.shape
        hidden = w_gate.shape[1]
        n_local, _, rank_dim = a_gate.shape
        n_hot = hot_ids.shape[0]
        cap = tok // (2 * group)
        half = tok // 2
        both = (n_hot + n_local) * rank_dim
        cfg = (group, cap, n_local, n_hot, rank_dim, LORA_ALPHA / rank_dim)

        def rows_of(a):
            return jnp.swapaxes(a, 1, 2).reshape(-1, a.shape[1])

        def flat(b):
            return b.reshape(-1, b.shape[2])

        any_spec = pl.BlockSpec(memory_space=pl.ANY)
        vmem_spec = pl.BlockSpec(memory_space=pltpu.VMEM)
        dma = pltpu.SemaphoreType.DMA
        place, back, kept = pl.pallas_call(
            functools.partial(main_kernel, cfg),
            out_shape=(
                jax.ShapeDtypeStruct((tok, 128), I32),
                jax.ShapeDtypeStruct((half, dim), BF16),
                jax.ShapeDtypeStruct((half, dim), BF16),
            ),
            in_specs=[vmem_spec, pl.BlockSpec(memory_space=pltpu.SMEM)] + [any_spec] * 16,
            out_specs=(vmem_spec, any_spec, any_spec),
            scratch_shapes=[
                pltpu.VMEM((tok, dim), BF16),
                pltpu.VMEM((tok, 128), BF16),
                pltpu.VMEM((half, dim), BF16),
                pltpu.VMEM((half, 128), BF16),
                pltpu.VMEM((half, hidden), BF16),
                pltpu.VMEM((half, hidden), BF16),
                pltpu.VMEM((both, dim), BF16),
                pltpu.VMEM((both, dim), BF16),
                pltpu.VMEM((both, hidden), BF16),
                pltpu.VMEM((both, dim), BF16),
                pltpu.VMEM((2, dim, GU_COLS), BF16),
                pltpu.VMEM((2, dim, GU_COLS), BF16),
                pltpu.VMEM((2, both, GU_COLS), BF16),
                pltpu.VMEM((2, both, GU_COLS), BF16),
                pltpu.VMEM((2, hidden, DN_COLS), BF16),
                pltpu.VMEM((half, both), BF16),
                pltpu.VMEM((half, both), BF16),
                pltpu.VMEM((half, both), BF16),
                dma((2,)), dma((2, 6)), dma((2,)), dma((8,)), dma((2,)),
                dma((group - 1,)), dma((group - 1,)), dma((group - 1,)), dma((group - 1,)),
                dma((dim // DN_COLS // 2, group - 1)), dma((dim // DN_COLS // 2, group - 1)),
            ],
            compiler_params=pltpu.CompilerParams(collective_id=0, has_side_effects=True, vmem_limit_bytes=66_000_000),
            name="mlp_exchange",
        )(adapter_id.reshape(1, tok), hot_ids, x, w_gate, w_up, w_down,
          rows_of(a_gate), flat(b_gate), rows_of(a_up), flat(b_up), rows_of(a_down), flat(b_down),
          rows_of(hot_a_gate), flat(hot_b_gate), rows_of(hot_a_up), flat(hot_b_up), rows_of(hot_a_down), flat(hot_b_down))

        block = 256
        return pl.pallas_call(
            unsort_kernel,
            grid=(tok // block,),
            out_shape=jax.ShapeDtypeStruct((tok, dim), BF16),
            in_specs=[
                pl.BlockSpec((block, 128), lambda i: (i, 0)),
                pl.BlockSpec((half, dim), lambda i: (0, 0)),
                pl.BlockSpec((half, dim), lambda i: (0, 0)),
            ],
            out_specs=pl.BlockSpec((block, dim), lambda i: (i, 0)),
            name="unsort",
        )(place, back, kept)

    return jax.shard_map(device_step, mesh=mesh, in_specs=in_specs, out_specs=token_spec, check_vma=False)
```

time: 464 us -> 149 us (0.32); the launches traced: 455 us -> 149 us
  matrix products: 161 us -> 0 us
  Pallas kernels: 0 us -> 149 us
  local copies, waits for them, and re-layouts: 89.3 us -> 0 us
  waiting for transfers between devices: 79.7 us -> 0 us
  blocking collectives: 69.4 us -> 0 us
  starting transfers between devices: 28.3 us -> 0 us
  other arithmetic: 27.1 us -> 0 us
    pallas_call x0 -> x2, Pallas kernels: none -> 149 us  [the longest x1 141 us: device_step(): pl.pallas_call(functools.partial(main_kernel, cfg), out_shape=(jax.ShapeD...]
    dot_general x9 -> x0, matrix products: 142 us -> none  [the longest x1 46.2 us: device_step(): jnp.dot(x, w_up, preferred_element_type=jnp.float32)]
    gather x11 -> x0, local copies, waits for them, and re-layouts: 84.7 us -> none  [the longest x3 52.9 us: to_tokens(): jnp.take(back_rows, tok_slot, axis=0).astype(jnp.float32)]
    all_to_all x5 -> x0, waiting for transfers between devices: 79.7 us -> none  [exchange(): return lax.all_to_all(send_rows, 'data', 0, 0, tiled=True)]
    all_to_all x1 -> x0, blocking collectives: 69.4 us -> none  [exchange(): return lax.all_to_all(send_rows, 'data', 0, 0, tiled=True)]
    all_to_all x5 -> x0, starting transfers between devices: 28.3 us -> none  [exchange(): return lax.all_to_all(send_rows, 'data', 0, 0, tiled=True)]
    unnamed x6 -> x0, matrix products: 18.8 us -> none
    select_n x7 -> x0, other arithmetic: 7.81 us -> none  [the longest x1 3.2 us: device_step(): recv_h = exchange(jnp.take(hidden, slot_tok, axis=0))]
  transfers between devices with their start and end apart: 5 -> 0, of which waited for: 4 -> 0; matrix products, arithmetic and copies ran while one was open for 25% -> 0% of each run, Pallas kernels for 0% -> 0%
where the time goes in v1:
time: 149 us
  Pallas kernels  149 us (100%)
    pallas_call x1, Pallas kernels, device_step(): pl.pallas_call(functools.partial(main_kernel, cfg), out_shape=(jax.ShapeD...  141 us
    pallas_call x1, Pallas kernels, device_step(): pl.pallas_call(unsort_kernel, grid=(tok // block,), out_shape=jax.ShapeDt...  8.39 us

profile of v1, /device:TPU:113, one launch (start us, length us, event | category | flops | bytes accessed | tf_op | source)
XLA Modules:
  0.0 149.1 jit_solution(4355771557939889833)
XLA Ops:
  0.0 140.7 %mlp_exchange.1 = (s32[1024,128]{1,0:T(8,128)}, bf16[512,2048]{1,0:T(8,128)(2,1)}, bf16[512,2048]{1,0:T(8,128)(2,1)}) custom-call(s32[1,1024]{1,0:T(1,128)} %bitcast.37, s32[4]{0:T(128)} %hot_ref.1, bf16[1024,2048]{1,0:T(8,128)(2,1)} %x_ref.1, bf16[2048,5632]{1,0:T(8,128)(2,1)} %wg_ref.1, bf16[2048,5632]{1,0:T(8,128)(2,1)} %wu_ref.1, ...), custom_call_target="tpu_custom_call" | custom-call | tf_op jit(solution)/shard_map/mlp_exchange/pallas_call | solution.py:286
  140.7 8.4 %unsort.1 = bf16[1024,2048]{1,0:T(8,128)(2,1)} custom-call(s32[1024,128]{1,0:T(8,128)} %get-tuple-element.8.place_ref, bf16[512,2048]{1,0:T(8,128)(2,1)} %get-tuple-element.9.back_ref, bf16[512,2048]{1,0:T(8,128)(2,1)} %get-tuple-element.10.kept_ref), custom_call_target="tpu_custom_call" | custom-call | tf_op jit(solution)/shard_map/unsort/pallas_call | solution.py:325

commit v2 on v1

--- a/solution.py
+++ b/solution.py
@@ -11,8 +11,9 @@
 BF16, F32, I32 = jnp.bfloat16, jnp.float32, jnp.int32
 MESH = pl.DeviceIdType.MESH
 GU_COLS = 512
-SUB_COLS = 256
-DN_COLS = 256
+SUB_ROWS = 256
+DN_COLS = 512
+LOAD_COLS = 512
 
 
 def nt_dot(rows, mat):
@@ -34,40 +35,43 @@
     owner = lax.div(ids, jnp.full(ids.shape, n_local, I32))
     slot = jnp.where(hot, slot, n_hot + ids - owner * n_local)
     key = jnp.where(hot, group, owner)
-    n_rows = -(-(group + 1) // 16) * 16
-    marks = (lax.broadcasted_iota(I32, (n_rows, tok), 0) == key).astype(F32)
+    rows = -(-(group + 1) // 16) * 16
     lane = 128
-    before = (lax.broadcasted_iota(I32, (lane, lane), 0) < lax.broadcasted_iota(I32, (lane, lane), 1)).astype(F32).astype(BF16)
-    total = jnp.zeros((n_rows, 1), F32)
+    blocks = tok // lane
+    marks = (lax.broadcasted_iota(I32, (rows, tok), 0) == key).astype(F32)
+    stacked = jnp.concatenate([marks[:, b * lane:(b + 1) * lane] for b in range(blocks)], axis=0).astype(BF16)
+    r, c = lax.broadcasted_iota(I32, (lane, 2 * lane), 0), lax.broadcasted_iota(I32, (lane, 2 * lane), 1)
+    counted = nn_dot(stacked, ((r < c) | (c >= lane)).astype(F32).astype(BF16))
+    total = jnp.zeros((rows, lane), F32)
     ranks = []
-    for b in range(tok // lane):
-        part = marks[:, b * lane:(b + 1) * lane]
-        ranks.append(nn_dot(part.astype(BF16), before) + total)
-        total = total + jnp.sum(part, axis=1, keepdims=True)
-    rank = jnp.concatenate(ranks, axis=1)
-    hot_rank = rank[group:group + 1, :]
-    spare = jnp.zeros((1, 1), F32)
-    place = jnp.zeros(ids.shape, F32)
-    placed = jnp.zeros(ids.shape, F32)
+    for b in range(blocks):
+        part = counted[b * rows:(b + 1) * rows, :]
+        ranks.append(part[:, :lane] + total)
+        total = total + part[:, lane:]
+    row = lax.broadcasted_iota(I32, (rows, lane), 0)
+    room = jnp.where(row < group, cap - total, 0.0)
+    before = jnp.zeros((rows, lane), F32)
     for j in range(group):
-        count = total[j:j + 1, :]
-        room = cap - count
-        cold_place = rank[j:j + 1, :] + float(j * cap)
-        place = jnp.where(key == j, cold_place, place)
-        fits = (key == group) & (hot_rank >= spare) & (hot_rank < spare + room)
-        place = jnp.where(fits, hot_rank - spare + (count + float(j * cap)), place)
-        placed = jnp.where(fits, 1.0, placed)
-        spare = spare + room
-    kept = (key == group) & (placed == 0.0)
-    place = jnp.where(kept, hot_rank - spare + float(group * cap), place)
-    return place, slot.astype(F32)
+        before = before + jnp.where(row > j, room[j:j + 1, :], 0.0)
+    base = row.astype(F32) * cap
+    all_room = before[group:group + 1, :]
+    places = []
+    for b in range(blocks):
+        mark, rank = marks[:, b * lane:(b + 1) * lane], ranks[b]
+        is_hot, hot_rank = mark[group:group + 1, :] > 0.0, rank[group:group + 1, :]
+        fits = is_hot & (row < group) & (hot_rank >= before) & (hot_rank < before + room)
+        spots = jnp.where(fits, hot_rank - before + total + base, 0.0)
+        spots = jnp.where((mark > 0.0) & (row < group), rank + base, spots)
+        place = jnp.sum(spots, axis=0, keepdims=True)
+        places.append(jnp.where(is_hot & (hot_rank >= all_room), hot_rank - all_room + group * cap, place))
+    return jnp.concatenate(places, axis=1), slot.astype(F32)
 
 
 def main_kernel(cfg, ids_ref, hot_ref, x_ref, wg_ref, wu_ref, wd_ref, ag_ref, bg_ref, au_ref, bu_ref, ad_ref, bd_ref,
                 hag_ref, hbg_ref, hau_ref, hbu_ref, had_ref, hbd_ref,
                 place_ref, back_ref, kept_ref,
-                xs, meta, recv, recv_meta, h_kept, h_recv, at_g, at_u, at_d, b_d, wg, wu, bg, bu, wd, low_g, low_u, low_d,
-                x_sem, w_sem, d_sem, a_sem, out_sem, send_sem, got_sem, msend_sem, mgot_sem, bsend_sem, bgot_sem):
+                xs, meta, recv, recv_meta, h_kept, h_recv, at_g, at_u, at_d, b_d, wg, wu, bg, bu, wd, low_g, low_u, low_d, place_t,
+                x_sem, w_sem, d_sem, a_sem, out_sem, send_sem, got_sem, msend_sem, mgot_sem, bsend_sem, bgot_sem, kept_sem):
     group, cap, n_local, n_hot, rank_dim, scale = cfg
     tok, dim = x_ref.shape
     hidden = wg_ref.shape[1]
@@ -82,7 +86,7 @@
 
     x_copies = [pltpu.make_async_copy(x_ref.at[pl.ds(i * half, half), :], h_recv.at[:, pl.ds(i * dim, dim)], x_sem.at[i]) for i in range(2)]
     for c in x_copies:
-        c.start()
+        c.start(priority=0)
     adapters = [
         pltpu.make_async_copy(hag_ref, at_g.at[pl.ds(0, hot_w), :], a_sem.at[0]),
         pltpu.make_async_copy(hau_ref, at_u.at[pl.ds(0, hot_w), :], a_sem.at[1]),
@@ -94,30 +98,33 @@
         pltpu.make_async_copy(bd_ref, b_d.at[pl.ds(hot_w, store_w), :], a_sem.at[7]),
     ]
 
-    def gu_copies(step):
-        cols = pl.ds(pl.multiple_of(lax.rem(step, gu_tiles) * GU_COLS, GU_COLS), GU_COLS)
-        s = lax.rem(step, 2)
+    def gu_place(step):
+        return pl.ds(pl.multiple_of(lax.rem(step, gu_tiles) * GU_COLS, GU_COLS), GU_COLS), lax.rem(step, 2)
+
+    def store_b_copies(step):
+        cols, s = gu_place(step)
+        return [
+            pltpu.make_async_copy(bg_ref.at[:, cols], bg.at[s, pl.ds(hot_w, store_w), :], w_sem.at[s, 4]),
+            pltpu.make_async_copy(bu_ref.at[:, cols], bu.at[s, pl.ds(hot_w, store_w), :], w_sem.at[s, 5]),
+        ]
+
+    def gu_copies(step, with_store):
+        cols, s = gu_place(step)
         return [
             pltpu.make_async_copy(wg_ref.at[:, cols], wg.at[s], w_sem.at[s, 0]),
             pltpu.make_async_copy(wu_ref.at[:, cols], wu.at[s], w_sem.at[s, 1]),
             pltpu.make_async_copy(hbg_ref.at[:, cols], bg.at[s, pl.ds(0, hot_w), :], w_sem.at[s, 2]),
             pltpu.make_async_copy(hbu_ref.at[:, cols], bu.at[s, pl.ds(0, hot_w), :], w_sem.at[s, 3]),
-            pltpu.make_async_copy(bg_ref.at[:, cols], bg.at[s, pl.ds(hot_w, store_w), :], w_sem.at[s, 4]),
-            pltpu.make_async_copy(bu_ref.at[:, cols], bu.at[s, pl.ds(hot_w, store_w), :], w_sem.at[s, 5]),
-        ]
+        ] + (store_b_copies(step) if with_store else [])
 
     def dn_copy(step):
         cols = pl.ds(pl.multiple_of(lax.rem(step, dn_tiles) * DN_COLS, DN_COLS), DN_COLS)
         s = lax.rem(step, 2)
-        return pltpu.make_async_copy(wd_ref.at[:, cols], wd.at[s], d_sem.at[s])
-
-    for c in adapters[:2]:
-        c.start()
-    for c in gu_copies(jnp.int32(0)):
-        c.start()
-    for c in adapters[2:]:
-        c.start()
-    dn_copy(jnp.int32(0)).start()
+        part = hidden // 2
+        return [pltpu.make_async_copy(wd_ref.at[pl.ds(j * part, part), cols], wd.at[s, pl.ds(j * part, part), :], d_sem.at[s, j]) for j in range(2)]
+
+    for c in adapters[:2] + gu_copies(jnp.int32(0), False):
+        c.start(priority=1)
 
     place, slot = route(ids_ref[...], hot_ref, group, n_local, n_hot, float(cap))
     place_i = place.astype(I32)
@@ -149,9 +156,14 @@
         for c in x_copy(k):
             c.start()
 
+    for c in adapters[2:] + dn_copy(jnp.int32(0)):
+        c.start(priority=1)
+
     sort_rows(512, 256)
     sort_rows(768, 256)
-    place_ref[...] = jnp.transpose(jnp.broadcast_to(place, (128, tok))).astype(I32)
+    place_t[...] = jnp.transpose(jnp.broadcast_to(place, (128, tok))).astype(I32)
+    place_out = pltpu.make_async_copy(place_t, place_ref, out_sem.at[1])
+    place_out.start()
     mine = pl.ds(pl.multiple_of(me * cap, cap), cap)
     recv[mine, :] = xs[mine, :]
     recv_meta[mine, :] = meta[mine, :]
@@ -171,20 +183,26 @@
         @pl.loop(0, gu_tiles)
         def _(i):
             step = i + first_step
-            for c in gu_copies(step):
+            for c in gu_copies(step, width > hot_w):
                 c.wait()
 
             @pl.when(step + 1 < 2 * gu_tiles)
             def _():
-                for c in gu_copies(step + 1):
-                    c.start()
+                for j, c in enumerate(gu_copies(step + 1, False)):
+                    c.start(priority=j % 2)
+
+            @pl.when((step + 1 >= gu_tiles) & (step + 1 < 2 * gu_tiles))
+            def _():
+                for j, c in enumerate(store_b_copies(step + 1)):
+                    c.start(priority=j % 2)
 
             s = lax.rem(step, 2)
-            for n in range(0, GU_COLS, SUB_COLS):
-                sub = slice(n, n + SUB_COLS)
-                g = nn_dot(rows_ref[rows, :], wg[s, :, sub]) + delta(low_g[:, :width], bg[s, :width, sub])
-                u = nn_dot(rows_ref[rows, :], wu[s, :, sub]) + delta(low_u[:, :width], bu[s, :width, sub])
-                h_ref[:, pl.ds(pl.multiple_of(i * GU_COLS + n, SUB_COLS), SUB_COLS)] = (jax.nn.silu(g) * u).astype(BF16)
+            cols = pl.ds(pl.multiple_of(i * GU_COLS, GU_COLS), GU_COLS)
+            for m in range(0, half, SUB_ROWS):
+                sub, src = slice(m, m + SUB_ROWS), slice(rows.start + m, rows.start + m + SUB_ROWS)
+                g = nn_dot(rows_ref[src, :], wg[s]) + delta(low_g[sub, :width], bg[s, :width, :])
+                u = nn_dot(rows_ref[src, :], wu[s]) + delta(low_u[sub, :width], bu[s, :width, :])
+                h_ref[sub, cols] = (jax.nn.silu(g) * u).astype(BF16)
 
     for c in adapters[:2]:
         c.wait()
@@ -200,7 +218,7 @@
 
     def back_copy(p, k):
         peer = lax.rem(me + k, group)
-        cols = pl.ds(pl.multiple_of(p * (2 * DN_COLS), 2 * DN_COLS), 2 * DN_COLS)
+        cols = pl.ds(pl.multiple_of(p * (DN_COLS), DN_COLS), DN_COLS)
         return pltpu.make_async_remote_copy(
             recv.at[pl.ds(pl.multiple_of(peer * cap, cap), cap), cols], back_ref.at[pl.ds(pl.multiple_of(me * cap, cap), cap), cols],
             bsend_sem.at[p, k - 1], bgot_sem.at[p, k - 1], device_id={"data": peer}, device_id_type=MESH)
@@ -208,20 +226,22 @@
     def down(h_ref, rows_ref, rows, slots, width, first_step, after):
         low_d[:, :width] = keep(nt_dot(h_ref[...], at_d[:width, :]), slots, width)
 
-        @pl.loop(0, dn_tiles // 2)
+        @pl.loop(0, dn_tiles)
         def _(p):
-            for q in range(2):
-                i = p * 2 + q
-                step = i + first_step
-                dn_copy(step).wait()
-
-                @pl.when(step + 1 < 2 * dn_tiles)
-                def _():
-                    dn_copy(step + 1).start()
-
-                cols = pl.ds(pl.multiple_of(i * DN_COLS, DN_COLS), DN_COLS)
-                y = nn_dot(h_ref[...], wd[lax.rem(step, 2)]) + delta(low_d[:, :width], b_d[:width, cols])
-                rows_ref[rows, cols] = (rows_ref[rows, cols].astype(F32) + y).astype(BF16)
+            step = p + first_step
+            for c in dn_copy(step):
+                c.wait()
+
+            @pl.when(step + 1 < 2 * dn_tiles)
+            def _():
+                for j, c in enumerate(dn_copy(step + 1)):
+                    c.start(priority=j)
+
+            cols = pl.ds(pl.multiple_of(p * DN_COLS, DN_COLS), DN_COLS)
+            for m in range(0, half, SUB_ROWS):
+                sub, src = slice(m, m + SUB_ROWS), slice(rows.start + m, rows.start + m + SUB_ROWS)
+                y = nn_dot(h_ref[sub, :], wd[lax.rem(step, 2)]) + delta(low_d[sub, :width], b_d[:width, cols])
+                rows_ref[src, cols] = (rows_ref[src, cols].astype(F32) + y).astype(BF16)
             after(p)
 
     def send_back(p):
@@ -231,29 +251,60 @@
     down(h_recv, recv, slice(0, half), recv_meta[...], hot_w + store_w, 0, send_back)
     own = pltpu.make_async_copy(recv.at[mine, :], back_ref.at[mine, :], out_sem.at[0])
     own.start()
-    down(h_kept, xs, kept_rows, meta[kept_rows, :], hot_w, dn_tiles, lambda p: None)
-    kept_out = pltpu.make_async_copy(xs.at[pl.ds(half, half), :], kept_ref, out_sem.at[1])
-    kept_out.start()
+
+    def kept_copy(p):
+        cols = pl.ds(pl.multiple_of(p * DN_COLS, DN_COLS), DN_COLS)
+        return pltpu.make_async_copy(xs.at[pl.ds(half, half), cols], kept_ref.at[:, cols], kept_sem.at[p])
+
+    down(h_kept, xs, kept_rows, meta[kept_rows, :], hot_w, dn_tiles, lambda p: kept_copy(p).start())
     own.wait()
-    kept_out.wait()
+    place_out.wait()
     for k in range(1, group):
         for c in x_copy(k):
             c.wait_send()
 
-    @pl.loop(0, dn_tiles // 2)
+    @pl.loop(0, dn_tiles)
     def _(p):
         for k in range(1, group):
             back_copy(p, k).wait()
-
-
-def unsort_kernel(place_ref, back_ref, kept_ref, out_ref):
-    count, half = out_ref.shape[0], back_ref.shape[0]
-    dim = out_ref.shape[1]
-    place = jnp.concatenate([place_ref[...]] * (2 * half // 128), axis=1)
-    sel = (place == lax.broadcasted_iota(I32, (count, 2 * half), 1)).astype(F32).astype(BF16)
-    for n in range(0, dim, 512):
-        rows = nn_dot(sel[:, :half], back_ref[:, n:n + 512]) + nn_dot(sel[:, half:], kept_ref[:, n:n + 512])
-        out_ref[:, n:n + 512] = rows.astype(BF16)
+        kept_copy(p).wait()
+
+
+def unsort_kernel(place_ref, back_ref, kept_ref, out_ref, place, rows, sel, done, sem, out_sem):
+    tok, dim = out_ref.shape
+    half = tok // 2
+
+    def load(n):
+        cols = pl.ds(n * LOAD_COLS, LOAD_COLS)
+        return [pltpu.make_async_copy(ref.at[:, cols], rows.at[pl.ds(j * half, half), cols], sem.at[n, j]) for j, ref in enumerate((back_ref, kept_ref))]
+
+    n_stores = (tok // 256) * (dim // LOAD_COLS)
+
+    def store(i):
+        n, t = divmod(i, tok // 256)
+        return pltpu.make_async_copy(done.at[i % 4], out_ref.at[pl.ds(t * 256, 256), pl.ds(n * LOAD_COLS, LOAD_COLS)], out_sem.at[i % 4])
+
+    first = pltpu.make_async_copy(place_ref, place, sem.at[dim // LOAD_COLS, 0])
+    first.start(priority=0)
+    for n in range(dim // LOAD_COLS):
+        for c in load(n):
+            c.start(priority=1)
+    first.wait()
+    for t in range(0, tok, 256):
+        spots = jnp.concatenate([place[t:t + 256, :]] * (tok // 128), axis=1)
+        sel[t:t + 256, :] = (spots == lax.broadcasted_iota(I32, (256, tok), 1)).astype(F32).astype(BF16)
+    for n in range(dim // LOAD_COLS):
+        for c in load(n):
+            c.wait()
+        cols = slice(n * LOAD_COLS, (n + 1) * LOAD_COLS)
+        for t in range(0, tok, 256):
+            i = n * (tok // 256) + t // 256
+            if i >= 4:
+                store(i - 4).wait()
+            done[i % 4] = (nn_dot(sel[t:t + 256, :half], rows[:half, cols]) + nn_dot(sel[t:t + 256, half:], rows[half:, cols])).astype(BF16)
+            store(i).start()
+    for i in range(n_stores - 4, n_stores):
+        store(i).wait()
 
 
 def solution(mesh):
@@ -291,7 +342,7 @@
                 jax.ShapeDtypeStruct((half, dim), BF16),
             ),
             in_specs=[vmem_spec, pl.BlockSpec(memory_space=pltpu.SMEM)] + [any_spec] * 16,
-            out_specs=(vmem_spec, any_spec, any_spec),
+            out_specs=(any_spec, any_spec, any_spec),
             scratch_shapes=[
                 pltpu.VMEM((tok, dim), BF16),
                 pltpu.VMEM((tok, 128), BF16),
@@ -311,9 +362,10 @@
                 pltpu.VMEM((half, both), BF16),
                 pltpu.VMEM((half, both), BF16),
                 pltpu.VMEM((half, both), BF16),
-                dma((2,)), dma((2, 6)), dma((2,)), dma((8,)), dma((2,)),
+                pltpu.VMEM((tok, 128), I32),
+                dma((2,)), dma((2, 6)), dma((2, 2)), dma((8,)), dma((2,)),
                 dma((group - 1,)), dma((group - 1,)), dma((group - 1,)), dma((group - 1,)),
-                dma((dim // DN_COLS // 2, group - 1)), dma((dim // DN_COLS // 2, group - 1)),
+                dma((dim // DN_COLS, group - 1)), dma((dim // DN_COLS, group - 1)), dma((dim // DN_COLS,)),
             ],
             compiler_params=pltpu.CompilerParams(collective_id=0, has_side_effects=True, vmem_limit_bytes=66_000_000),
             name="mlp_exchange",
@@ -321,17 +373,19 @@
           rows_of(a_gate), flat(b_gate), rows_of(a_up), flat(b_up), rows_of(a_down), flat(b_down),
           rows_of(hot_a_gate), flat(hot_b_gate), rows_of(hot_a_up), flat(hot_b_up), rows_of(hot_a_down), flat(hot_b_down))
 
-        block = 256
         return pl.pallas_call(
             unsort_kernel,
-            grid=(tok // block,),
             out_shape=jax.ShapeDtypeStruct((tok, dim), BF16),
-            in_specs=[
-                pl.BlockSpec((block, 128), lambda i: (i, 0)),
-                pl.BlockSpec((half, dim), lambda i: (0, 0)),
-                pl.BlockSpec((half, dim), lambda i: (0, 0)),
+            in_specs=[any_spec] * 3,
+            out_specs=any_spec,
+            scratch_shapes=[
+                pltpu.VMEM((tok, 128), I32),
+                pltpu.VMEM((tok, dim), BF16),
+                pltpu.VMEM((tok, tok), BF16),
+                pltpu.VMEM((4, 256, LOAD_COLS), BF16),
+                dma((dim // LOAD_COLS + 1, 2)),
+                dma((4,)),
             ],
-            out_specs=pl.BlockSpec((block, dim), lambda i: (i, 0)),
             name="unsort",
         )(place, back, kept)
 

time: 149 us -> 119 us (0.80)
  Pallas kernels: 149 us -> 119 us
    pallas_call x1, Pallas kernels: 141 us -> 110 us  [device_step(): pl.pallas_call(functools.partial(main_kernel, cfg), out_shape=(jax.ShapeD...]
where the time goes in v2:
time: 119 us
  Pallas kernels  119 us (100%)
    pallas_call x1, Pallas kernels, device_step(): pl.pallas_call(functools.partial(main_kernel, cfg), out_shape=(jax.ShapeD...  110 us
    pallas_call x1, Pallas kernels, device_step(): pl.pallas_call(unsort_kernel, out_shape=jax.ShapeDtypeStruct((tok, dim),...  8.95 us

profile of v2, /device:TPU:113, one launch (start us, length us, event | category | flops | bytes accessed | tf_op | source)
XLA Modules:
  0.0 118.7 jit_solution(7172312307022806030)
XLA Ops:
  0.0 109.6 %mlp_exchange.1 = (s32[1024,128]{1,0:T(8,128)}, bf16[512,2048]{1,0:T(8,128)(2,1)}, bf16[512,2048]{1,0:T(8,128)(2,1)}) custom-call(s32[1,1024]{1,0:T(1,128)} %bitcast.37, s32[4]{0:T(128)} %hot_ref.1, bf16[1024,2048]{1,0:T(8,128)(2,1)} %x_ref.1, bf16[2048,5632]{1,0:T(8,128)(2,1)} %wg_ref.1, bf16[2048,5632]{1,0:T(8,128)(2,1)} %wu_ref.1, ...), custom_call_target="tpu_custom_call" | custom-call | tf_op jit(solution)/shard_map/mlp_exchange/pallas_call | solution.py:337
  109.6 9.0 %unsort.1 = bf16[1024,2048]{1,0:T(8,128)(2,1)} custom-call(s32[1024,128]{1,0:T(8,128)} %get-tuple-element.8.place_ref, bf16[512,2048]{1,0:T(8,128)(2,1)} %get-tuple-element.9.back_ref, bf16[512,2048]{1,0:T(8,128)(2,1)} %get-tuple-element.10.kept_ref), custom_call_target="tpu_custom_call" | custom-call | tf_op jit(solution)/shard_map/unsort/pallas_call | solution.py:376

commit v3 on v2

v3 whole, which is shorter than its diff:
```python
import functools

import jax
import jax.numpy as jnp
from jax import lax
from jax.experimental import pallas as pl
from jax.experimental.pallas import tpu as pltpu
from jax.sharding import PartitionSpec as P

LORA_ALPHA = 32
BF16, F32, I32 = jnp.bfloat16, jnp.float32, jnp.int32
MESH = pl.DeviceIdType.MESH
BLOCK = 512
SUB_ROWS = 256
UNSORT_COLS = 256


def nt_dot(rows, mat):
    return lax.dot_general(rows, mat, (((1,), (1,)), ((), ())), preferred_element_type=F32)


def nn_dot(rows, mat):
    return jnp.dot(rows, mat, preferred_element_type=F32)


def route(ids, hot_ids_ref, group, n_local, n_hot, cap):
    tok = ids.shape[1]
    hot = jnp.zeros(ids.shape, jnp.bool_)
    slot = jnp.zeros(ids.shape, I32)
    for j in range(n_hot):
        match = ids == hot_ids_ref[j]
        hot = hot | match
        slot = jnp.where(match, j, slot)
    owner = lax.div(ids, jnp.full(ids.shape, n_local, I32))
    slot = jnp.where(hot, slot, n_hot + ids - owner * n_local)
    key = jnp.where(hot, group, owner)
    rows = -(-(group + 1) // 16) * 16
    lane = 128
    blocks = tok // lane
    marks = (lax.broadcasted_iota(I32, (rows, tok), 0) == key).astype(F32)
    stacked = jnp.concatenate([marks[:, b * lane:(b + 1) * lane] for b in range(blocks)], axis=0).astype(BF16)
    r, c = lax.broadcasted_iota(I32, (lane, 2 * lane), 0), lax.broadcasted_iota(I32, (lane, 2 * lane), 1)
    counted = nn_dot(stacked, ((r < c) | (c >= lane)).astype(F32).astype(BF16))
    total = jnp.zeros((rows, lane), F32)
    ranks = []
    for b in range(blocks):
        part = counted[b * rows:(b + 1) * rows, :]
        ranks.append(part[:, :lane] + total)
        total = total + part[:, lane:]
    row = lax.broadcasted_iota(I32, (rows, lane), 0)
    room = jnp.where(row < group, cap - total, 0.0)
    before = jnp.zeros((rows, lane), F32)
    for j in range(group):
        before = before + jnp.where(row > j, room[j:j + 1, :], 0.0)
    base = row.astype(F32) * cap
    all_room = before[group:group + 1, :]
    places = []
    for b in range(blocks):
        mark, rank = marks[:, b * lane:(b + 1) * lane], ranks[b]
        is_hot, hot_rank = mark[group:group + 1, :] > 0.0, rank[group:group + 1, :]
        fits = is_hot & (row < group) & (hot_rank >= before) & (hot_rank < before + room)
        spots = jnp.where(fits, hot_rank - before + total + base, 0.0)
        spots = jnp.where((mark > 0.0) & (row < group), rank + base, spots)
        place = jnp.sum(spots, axis=0, keepdims=True)
        places.append(jnp.where(is_hot & (hot_rank >= all_room), hot_rank - all_room + group * cap, place))
    return jnp.concatenate(places, axis=1), slot.astype(F32)


def main_kernel(cfg, ids_ref, hot_ref, x_ref, wg_ref, wu_ref, wd_ref, ag_ref, bg_ref, au_ref, bu_ref, ad_ref, bd_ref,
                hag_ref, hbg_ref, hau_ref, hbu_ref, had_ref, hbd_ref,
                place_ref, back_ref, kept_ref,
                xs, meta, recv, recv_meta, h_kept, h_recv, at_g, at_u, at_d, b_d, arena, low_g, low_u, low_d, place_t,
                x_sem, w_sem, d_sem, a_sem, out_sem, send_sem, got_sem, msend_sem, mgot_sem, bsend_sem, bgot_sem, kept_sem):
    group, cap, n_local, n_hot, rank_dim, scale = cfg
    tok, dim = x_ref.shape
    hidden = wg_ref.shape[1]
    half = tok // 2
    hot_w, store_w = n_hot * rank_dim, n_local * rank_dim
    gu_tiles, dn_tiles = hidden // BLOCK, dim // BLOCK
    gu_pairs, both = gu_tiles // 2, hot_w + store_w
    me = lax.axis_index("data")

    barrier = pltpu.get_barrier_semaphore()
    for k in range(1, group):
        pl.semaphore_signal(barrier, inc=1, device_id={"data": lax.rem(me + k, group)}, device_id_type=MESH)

    x_copies = [pltpu.make_async_copy(x_ref.at[pl.ds(i * half, half), pl.ds(n, BLOCK)], h_recv.at[:, pl.ds(i * dim + n, BLOCK)], x_sem.at[n // BLOCK, i])
                for n in range(0, dim, BLOCK) for i in range(2)]
    for c in x_copies:
        c.start(priority=0)
    adapters = [
        pltpu.make_async_copy(hag_ref, at_g.at[pl.ds(0, hot_w), :], a_sem.at[0]),
        pltpu.make_async_copy(hau_ref, at_u.at[pl.ds(0, hot_w), :], a_sem.at[1]),
        pltpu.make_async_copy(ag_ref, at_g.at[pl.ds(hot_w, store_w), :], a_sem.at[2]),
        pltpu.make_async_copy(au_ref, at_u.at[pl.ds(hot_w, store_w), :], a_sem.at[3]),
        pltpu.make_async_copy(had_ref, at_d.at[pl.ds(0, hot_w), :], a_sem.at[4]),
        pltpu.make_async_copy(ad_ref, at_d.at[pl.ds(hot_w, store_w), :], a_sem.at[5]),
        pltpu.make_async_copy(hbd_ref, b_d.at[pl.ds(0, hot_w), :], a_sem.at[6]),
        pltpu.make_async_copy(bd_ref, b_d.at[pl.ds(hot_w, store_w), :], a_sem.at[7]),
    ]

    g_row, u_row = 0, 2 * dim
    bg_row, bu_row = 4 * dim, 4 * dim + 2 * both

    def gu_copies(pair, s, with_store):
        copies = []
        for q in range(2):
            cols = pl.ds(pl.multiple_of(lax.rem(2 * pair + q, gu_tiles) * BLOCK, BLOCK), BLOCK)
            parts = [(wg_ref, g_row + q * dim, dim), (wu_ref, u_row + q * dim, dim),
                     (hbg_ref, bg_row + q * both, hot_w), (hbu_ref, bu_row + q * both, hot_w)]
            if with_store:
                parts += [(bg_ref, bg_row + q * both + hot_w, store_w), (bu_ref, bu_row + q * both + hot_w, store_w)]
            for j, (ref, first, count) in enumerate(parts):
                copies.append(pltpu.make_async_copy(ref.at[:, cols], arena.at[s, pl.ds(first, count), :], w_sem.at[s, q, j]))
        return copies

    def dn_copies(pair, s):
        copies = []
        for q in range(2):
            cols = pl.ds(pl.multiple_of(lax.rem(2 * pair + q, dn_tiles) * BLOCK, BLOCK), BLOCK)
            copies.append(pltpu.make_async_copy(wd_ref.at[:, cols], arena.at[s, pl.ds(q * hidden, hidden), :], d_sem.at[s, q]))
        return copies

    def start(copies):
        for j, c in enumerate(copies):
            c.start(priority=j % 2)

    def wait(copies):
        for c in copies:
            c.wait()

    for c in adapters[:2] + gu_copies(0, 0, False):
        c.start(priority=1)

    place, slot = route(ids_ref[...], hot_ref, group, n_local, n_hot, float(cap))
    place_i = place.astype(I32)
    slot_b = jnp.broadcast_to(slot, (128, tok)).astype(BF16)
    def sort_rows(first, arrive):
        sels = []
        for m in range(first, first + half, SUB_ROWS):
            sel = (lax.broadcasted_iota(I32, (SUB_ROWS, tok), 0) + m == place_i).astype(F32).astype(BF16)
            meta[pl.ds(m, SUB_ROWS), :] = nt_dot(sel, slot_b).astype(BF16)
            sels.append(sel)
        for n in range(0, dim, BLOCK):
            if arrive:
                for i in range(2):
                    x_copies[n // BLOCK * 2 + i].wait()
            for j, sel in enumerate(sels):
                rows = nn_dot(sel[:, :half], h_recv[:, n:n + BLOCK]) + nn_dot(sel[:, half:], h_recv[:, dim + n:dim + n + BLOCK])
                xs[pl.ds(first + j * SUB_ROWS, SUB_ROWS), n:n + BLOCK] = rows.astype(BF16)

    sort_rows(0, True)

    pl.semaphore_wait(barrier, group - 1)

    def x_copy(k):
        peer = lax.rem(me + k, group)
        src, dst = pl.ds(pl.multiple_of(peer * cap, cap), cap), pl.ds(pl.multiple_of(me * cap, cap), cap)
        return (
            pltpu.make_async_remote_copy(xs.at[src, :], recv.at[dst, :], send_sem.at[k - 1], got_sem.at[k - 1], device_id={"data": peer}, device_id_type=MESH),
            pltpu.make_async_remote_copy(meta.at[src, :], recv_meta.at[dst, :], msend_sem.at[k - 1], mgot_sem.at[k - 1], device_id={"data": peer}, device_id_type=MESH),
        )

    for k in range(1, group):
        for c in x_copy(k):
            c.start()

    for c in adapters[2:]:
        c.start(priority=1)

    sort_rows(half, False)
    place_t[...] = jnp.transpose(jnp.broadcast_to(place, (128, tok))).astype(I32)
    place_out = pltpu.make_async_copy(place_t, place_ref, out_sem.at[1])
    place_out.start()
    mine = pl.ds(pl.multiple_of(me * cap, cap), cap)
    recv[mine, :] = xs[mine, :]
    recv_meta[mine, :] = meta[mine, :]

    def keep(low, slots, width):
        cols = jnp.concatenate([slots.astype(F32)] * (width // 128), axis=1)
        lanes = lax.div(lax.broadcasted_iota(I32, cols.shape, 1), jnp.full(cols.shape, rank_dim, I32)).astype(F32)
        return jnp.where(cols == lanes, low, 0.0).astype(BF16)

    def delta(low, mat):
        return (scale * nn_dot(low, mat)).astype(BF16).astype(F32)

    def gate_up(rows_ref, rows, slots, width, h_ref, start_next):
        low_g[:, :width] = keep(nt_dot(rows_ref[rows, :], at_g[:width, :]), slots, width)
        low_u[:, :width] = keep(nt_dot(rows_ref[rows, :], at_u[:width, :]), slots, width)
        with_store = width > hot_w

        def block(tile, s, q):
            cols = pl.ds(pl.multiple_of(tile * BLOCK, BLOCK), BLOCK)
            for m in range(0, half, SUB_ROWS):
                sub, src = slice(m, m + SUB_ROWS), slice(rows.start + m, rows.start + m + SUB_ROWS)
                g = nn_dot(rows_ref[src, :], arena[s, g_row + q * dim:g_row + (q + 1) * dim, :])
                g = g + delta(low_g[sub, :width], arena[s, bg_row + q * both:bg_row + q * both + width, :])
                u = nn_dot(rows_ref[src, :], arena[s, u_row + q * dim:u_row + (q + 1) * dim, :])
                u = u + delta(low_u[sub, :width], arena[s, bu_row + q * both:bu_row + q * both + width, :])
                h_ref[sub, cols] = (jax.nn.silu(g) * u).astype(BF16)

        @pl.loop(0, gu_pairs)
        def _(i):
            s = lax.rem(i, 2)
            wait(gu_copies(i, s, with_store))
            start(gu_copies(i + 1, 1 - s, with_store))
            for q in range(2):
                block(2 * i + q, s, q)

        s = gu_pairs % 2
        wait(gu_copies(gu_pairs, s, with_store))
        start_next()
        block(gu_tiles - 1, s, 0)

    for c in adapters[:2]:
        c.wait()
    kept_rows = slice(half, tok)
    gate_up(xs, kept_rows, meta[kept_rows, :], hot_w, h_kept, lambda: start(gu_copies(0, 0, True)))

    for c in adapters[2:]:
        c.wait()
    for k in range(1, group):
        for c in x_copy(k):
            c.wait_recv()
    gate_up(recv, slice(0, half), recv_meta[...], both, h_recv, lambda: start(dn_copies(0, 0)))

    def back_copy(p, k):
        peer = lax.rem(me + k, group)
        cols = pl.ds(pl.multiple_of(p * (BLOCK), BLOCK), BLOCK)
        return pltpu.make_async_remote_copy(
            recv.at[pl.ds(pl.multiple_of(peer * cap, cap), cap), cols], back_ref.at[pl.ds(pl.multiple_of(me * cap, cap), cap), cols],
            bsend_sem.at[p, k - 1], bgot_sem.at[p, k - 1], device_id={"data": peer}, device_id_type=MESH)

    def down(h_ref, rows_ref, rows, slots, width, after):
        low_d[:, :width] = keep(nt_dot(h_ref[...], at_d[:width, :]), slots, width)

        @pl.loop(0, dn_tiles // 2)
        def _(i):
            s = lax.rem(i, 2)
            wait(dn_copies(i, s))
            start(dn_copies(i + 1, 1 - s))
            for q in range(2):
                p = 2 * i + q
                cols = pl.ds(pl.multiple_of(p * BLOCK, BLOCK), BLOCK)
                for m in range(0, half, SUB_ROWS):
                    sub, src = slice(m, m + SUB_ROWS), slice(rows.start + m, rows.start + m + SUB_ROWS)
                    y = nn_dot(h_ref[sub, :], arena[s, q * hidden:(q + 1) * hidden, :]) + delta(low_d[sub, :width], b_d[:width, cols])
                    rows_ref[src, cols] = (rows_ref[src, cols].astype(F32) + y).astype(BF16)
                after(p)

    def send_back(p):
        for k in range(1, group):
            back_copy(p, k).start()

    down(h_recv, recv, slice(0, half), recv_meta[...], both, send_back)
    own = pltpu.make_async_copy(recv.at[mine, :], back_ref.at[mine, :], out_sem.at[0])
    own.start()

    def kept_copy(p):
        cols = pl.ds(pl.multiple_of(p * BLOCK, BLOCK), BLOCK)
        return pltpu.make_async_copy(xs.at[pl.ds(half, half), cols], kept_ref.at[:, cols], kept_sem.at[p])

    down(h_kept, xs, kept_rows, meta[kept_rows, :], hot_w, lambda p: kept_copy(p).start())
    wait(dn_copies(0, 0))
    own.wait()
    place_out.wait()
    for k in range(1, group):
        for c in x_copy(k):
            c.wait_send()

    @pl.loop(0, dn_tiles)
    def _(p):
        for k in range(1, group):
            back_copy(p, k).wait()
        kept_copy(p).wait()


def unsort_kernel(place_ref, back_ref, kept_ref, out_ref, sel):
    tok, half = out_ref.shape[0], back_ref.shape[0]

    @pl.when(pl.program_id(0) == 0)
    def _():
        place = jnp.concatenate([place_ref[...]] * (tok // 128), axis=1)
        sel[...] = (place == lax.broadcasted_iota(I32, (tok, tok), 1)).astype(F32).astype(BF16)

    for n in range(0, out_ref.shape[1], UNSORT_COLS):
        cols = slice(n, n + UNSORT_COLS)
        rows = nn_dot(sel[:, :half], back_ref[:, cols]) + nn_dot(sel[:, half:], kept_ref[:, cols])
        out_ref[:, cols] = rows.astype(BF16)


def solution(mesh):
    group = mesh.shape["data"]
    token_spec = P(("replica", "data"), None)
    store_spec = P("data", None, None)
    full_mat = P(None, None)
    full_set = P(None, None, None)
    in_specs = (token_spec, P(("replica", "data")), full_mat, full_mat, full_mat) + (store_spec,) * 6 + (P(None),) + (full_set,) * 6

    def device_step(x, adapter_id, w_gate, w_up, w_down, a_gate, b_gate, a_up, b_up, a_down, b_down, hot_ids, hot_a_gate, hot_b_gate, hot_a_up, hot_b_up, hot_a_down, hot_b_down):
        tok, dim = x.shape
        hidden = w_gate.shape[1]
        n_local, _, rank_dim = a_gate.shape
        n_hot = hot_ids.shape[0]
        cap = tok // (2 * group)
        half = tok // 2
        both = (n_hot + n_local) * rank_dim
        cfg = (group, cap, n_local, n_hot, rank_dim, LORA_ALPHA / rank_dim)

        def rows_of(a):
            return jnp.swapaxes(a, 1, 2).reshape(-1, a.shape[1])

        def flat(b):
            return b.reshape(-1, b.shape[2])

        any_spec = pl.BlockSpec(memory_space=pl.ANY)
        vmem_spec = pl.BlockSpec(memory_space=pltpu.VMEM)
        dma = pltpu.SemaphoreType.DMA
        place, back, kept = pl.pallas_call(
            functools.partial(main_kernel, cfg),
            out_shape=(
                jax.ShapeDtypeStruct((tok, 128), I32),
                jax.ShapeDtypeStruct((half, dim), BF16),
                jax.ShapeDtypeStruct((half, dim), BF16),
            ),
            in_specs=[vmem_spec, pl.BlockSpec(memory_space=pltpu.SMEM)] + [any_spec] * 16,
            out_specs=(any_spec, any_spec, any_spec),
            scratch_shapes=[
                pltpu.VMEM((tok, dim), BF16),
                pltpu.VMEM((tok, 128), BF16),
                pltpu.VMEM((half, dim), BF16),
                pltpu.VMEM((half, 128), BF16),
                pltpu.VMEM((half, hidden), BF16),
                pltpu.VMEM((half, hidden), BF16),
                pltpu.VMEM((both, dim), BF16),
                pltpu.VMEM((both, dim), BF16),
                pltpu.VMEM((both, hidden), BF16),
                pltpu.VMEM((both, dim), BF16),
                pltpu.VMEM((2, max(4 * dim + 4 * both, 2 * hidden), BLOCK), BF16),
                pltpu.VMEM((half, both), BF16),
                pltpu.VMEM((half, both), BF16),
                pltpu.VMEM((half, both), BF16),
                pltpu.VMEM((tok, 128), I32),
                dma((dim // BLOCK, 2)), dma((2, 2, 6)), dma((2, 2)), dma((8,)), dma((2,)),
                dma((group - 1,)), dma((group - 1,)), dma((group - 1,)), dma((group - 1,)),
                dma((dim // BLOCK, group - 1)), dma((dim // BLOCK, group - 1)), dma((dim // BLOCK,)),
            ],
            compiler_params=pltpu.CompilerParams(collective_id=0, has_side_effects=True, vmem_limit_bytes=66_000_000),
            name="mlp_exchange",
        )(adapter_id.reshape(1, tok), hot_ids, x, w_gate, w_up, w_down,
          rows_of(a_gate), flat(b_gate), rows_of(a_up), flat(b_up), rows_of(a_down), flat(b_down),
          rows_of(hot_a_gate), flat(hot_b_gate), rows_of(hot_a_up), flat(hot_b_up), rows_of(hot_a_down), flat(hot_b_down))

        block = 512
        return pl.pallas_call(
            unsort_kernel,
            grid=(dim // block,),
            out_shape=jax.ShapeDtypeStruct((tok, dim), BF16),
            in_specs=[
                pl.BlockSpec((tok, 128), lambda i: (0, 0)),
                pl.BlockSpec((half, block), lambda i: (0, i)),
                pl.BlockSpec((half, block), lambda i: (0, i)),
            ],
            out_specs=pl.BlockSpec((tok, block), lambda i: (0, i)),
            scratch_shapes=[pltpu.VMEM((tok, tok), BF16)],
            name="unsort",
        )(place, back, kept)

    return jax.shard_map(device_step, mesh=mesh, in_specs=in_specs, out_specs=token_spec, check_vma=False)
```

time: 119 us -> 115 us (0.966)
  Pallas kernels: 119 us -> 115 us
    pallas_call x1, Pallas kernels: 110 us -> 107 us  [device_step(): pl.pallas_call(functools.partial(main_kernel, cfg), out_shape=(jax.ShapeD...]
where the time goes in v3:
time: 115 us
  Pallas kernels  115 us (100%)
    pallas_call x1, Pallas kernels, device_step(): pl.pallas_call(functools.partial(main_kernel, cfg), out_shape=(jax.ShapeD...  107 us
    pallas_call x1, Pallas kernels, device_step(): pl.pallas_call(unsort_kernel, grid=(dim // block,), out_shape=jax.ShapeDt...  8.13 us

profile of v3, /device:TPU:113, one launch (start us, length us, event | category | flops | bytes accessed | tf_op | source)
XLA Modules:
  0.0 114.9 jit_solution(2968173004274507284)
XLA Ops:
  0.0 106.7 %mlp_exchange.1 = (s32[1024,128]{1,0:T(8,128)}, bf16[512,2048]{1,0:T(8,128)(2,1)}, bf16[512,2048]{1,0:T(8,128)(2,1)}) custom-call(s32[1,1024]{1,0:T(1,128)} %bitcast.37, s32[4]{0:T(128)} %hot_ref.1, bf16[1024,2048]{1,0:T(8,128)(2,1)} %x_ref.1, bf16[2048,5632]{1,0:T(8,128)(2,1)} %wg_ref.1, bf16[2048,5632]{1,0:T(8,128)(2,1)} %wu_ref.1, ...), custom_call_target="tpu_custom_call" | custom-call | tf_op jit(solution)/shard_map/mlp_exchange/pallas_call | solution.py:319
  106.7 8.1 %unsort.1 = bf16[1024,2048]{1,0:T(8,128)(2,1)} custom-call(s32[1024,128]{1,0:T(8,128)} %get-tuple-element.8.place_ref, bf16[512,2048]{1,0:T(8,128)(2,1)} %get-tuple-element.9.back_ref, bf16[512,2048]{1,0:T(8,128)(2,1)} %get-tuple-element.10.kept_ref), custom_call_target="tpu_custom_call" | custom-call | tf_op jit(solution)/shard_map/unsort/pallas_call | solution.py:355

commit v4 on v3

--- a/solution.py
+++ b/solution.py
@@ -12,7 +12,6 @@
 MESH = pl.DeviceIdType.MESH
 BLOCK = 512
 SUB_ROWS = 256
-UNSORT_COLS = 256
 
 
 def nt_dot(rows, mat):
@@ -193,10 +192,10 @@
             cols = pl.ds(pl.multiple_of(tile * BLOCK, BLOCK), BLOCK)
             for m in range(0, half, SUB_ROWS):
                 sub, src = slice(m, m + SUB_ROWS), slice(rows.start + m, rows.start + m + SUB_ROWS)
-                g = nn_dot(rows_ref[src, :], arena[s, g_row + q * dim:g_row + (q + 1) * dim, :])
-                g = g + delta(low_g[sub, :width], arena[s, bg_row + q * both:bg_row + q * both + width, :])
-                u = nn_dot(rows_ref[src, :], arena[s, u_row + q * dim:u_row + (q + 1) * dim, :])
-                u = u + delta(low_u[sub, :width], arena[s, bu_row + q * both:bu_row + q * both + width, :])
+                add_g = delta(low_g[sub, :width], arena[s, bg_row + q * both:bg_row + q * both + width, :])
+                g = nn_dot(rows_ref[src, :], arena[s, g_row + q * dim:g_row + (q + 1) * dim, :]) + add_g
+                add_u = delta(low_u[sub, :width], arena[s, bu_row + q * both:bu_row + q * both + width, :])
+                u = nn_dot(rows_ref[src, :], arena[s, u_row + q * dim:u_row + (q + 1) * dim, :]) + add_u
                 h_ref[sub, cols] = (jax.nn.silu(g) * u).astype(BF16)
 
         @pl.loop(0, gu_pairs)
@@ -244,7 +243,8 @@
                 cols = pl.ds(pl.multiple_of(p * BLOCK, BLOCK), BLOCK)
                 for m in range(0, half, SUB_ROWS):
                     sub, src = slice(m, m + SUB_ROWS), slice(rows.start + m, rows.start + m + SUB_ROWS)
-                    y = nn_dot(h_ref[sub, :], arena[s, q * hidden:(q + 1) * hidden, :]) + delta(low_d[sub, :width], b_d[:width, cols])
+                    add_y = delta(low_d[sub, :width], b_d[:width, cols])
+                    y = nn_dot(h_ref[sub, :], arena[s, q * hidden:(q + 1) * hidden, :]) + add_y
                     rows_ref[src, cols] = (rows_ref[src, cols].astype(F32) + y).astype(BF16)
                 after(p)
 
@@ -275,18 +275,38 @@
         kept_copy(p).wait()
 
 
-def unsort_kernel(place_ref, back_ref, kept_ref, out_ref, sel):
-    tok, half = out_ref.shape[0], back_ref.shape[0]
-
-    @pl.when(pl.program_id(0) == 0)
-    def _():
-        place = jnp.concatenate([place_ref[...]] * (tok // 128), axis=1)
-        sel[...] = (place == lax.broadcasted_iota(I32, (tok, tok), 1)).astype(F32).astype(BF16)
-
-    for n in range(0, out_ref.shape[1], UNSORT_COLS):
-        cols = slice(n, n + UNSORT_COLS)
-        rows = nn_dot(sel[:, :half], back_ref[:, cols]) + nn_dot(sel[:, half:], kept_ref[:, cols])
-        out_ref[:, cols] = rows.astype(BF16)
+def unsort_kernel(place_ref, back_ref, kept_ref, out_ref, place, rows, sel, done, place_sem, sem, out_sem):
+    tok, dim = out_ref.shape
+    half = tok // 2
+    parts = dim // BLOCK
+
+    def load(n):
+        cols = pl.ds(n * BLOCK, BLOCK)
+        return [pltpu.make_async_copy(ref.at[:, cols], rows.at[pl.ds(j * half, half), cols], sem.at[n, j]) for j, ref in enumerate((back_ref, kept_ref))]
+
+    def store(n):
+        return pltpu.make_async_copy(done.at[n % 2], out_ref.at[:, pl.ds(n * BLOCK, BLOCK)], out_sem.at[n % 2])
+
+    first = pltpu.make_async_copy(place_ref, place, place_sem.at[0])
+    first.start(priority=0)
+    loads = [load(n) for n in range(parts)]
+    for copies in loads:
+        for c in copies:
+            c.start(priority=1)
+    first.wait()
+    for t in range(0, tok, SUB_ROWS):
+        spots = jnp.concatenate([place[t:t + SUB_ROWS, :]] * (tok // 128), axis=1)
+        sel[t:t + SUB_ROWS, :] = (spots == lax.broadcasted_iota(I32, (SUB_ROWS, tok), 1)).astype(F32).astype(BF16)
+    for n in range(parts):
+        for c in loads[n]:
+            c.wait()
+        if n >= 2:
+            store(n - 2).wait()
+        cols = slice(n * BLOCK, (n + 1) * BLOCK)
+        done[n % 2] = (nn_dot(sel[:, :half], rows[:half, cols]) + nn_dot(sel[:, half:], rows[half:, cols])).astype(BF16)
+        store(n).start()
+    for n in range(max(parts - 2, 0), parts):
+        store(n).wait()
 
 
 def solution(mesh):
@@ -351,18 +371,20 @@
           rows_of(a_gate), flat(b_gate), rows_of(a_up), flat(b_up), rows_of(a_down), flat(b_down),
           rows_of(hot_a_gate), flat(hot_b_gate), rows_of(hot_a_up), flat(hot_b_up), rows_of(hot_a_down), flat(hot_b_down))
 
-        block = 512
         return pl.pallas_call(
             unsort_kernel,
-            grid=(dim // block,),
             out_shape=jax.ShapeDtypeStruct((tok, dim), BF16),
-            in_specs=[
-                pl.BlockSpec((tok, 128), lambda i: (0, 0)),
-                pl.BlockSpec((half, block), lambda i: (0, i)),
-                pl.BlockSpec((half, block), lambda i: (0, i)),
+            in_specs=[any_spec] * 3,
+            out_specs=any_spec,
+            scratch_shapes=[
+                pltpu.VMEM((tok, 128), I32),
+                pltpu.VMEM((tok, dim), BF16),
+                pltpu.VMEM((tok, tok), BF16),
+                pltpu.VMEM((2, tok, BLOCK), BF16),
+                dma((1,)),
+                dma((dim // BLOCK, 2)),
+                dma((2,)),
             ],
-            out_specs=pl.BlockSpec((tok, block), lambda i: (0, i)),
-            scratch_shapes=[pltpu.VMEM((tok, tok), BF16)],
             name="unsort",
         )(place, back, kept)
 

time: 115 us -> 115 us (level)
  no operation moved by 1% of the time
where the time goes in v4:
time: 115 us
  Pallas kernels  115 us (100%)
    pallas_call x1, Pallas kernels, device_step(): pl.pallas_call(functools.partial(main_kernel, cfg), out_shape=(jax.ShapeD...  107 us
    pallas_call x1, Pallas kernels, device_step(): pl.pallas_call(unsort_kernel, out_shape=jax.ShapeDtypeStruct((tok, dim),...  7.78 us

profile of v4, /device:TPU:113, one launch (start us, length us, event | category | flops | bytes accessed | tf_op | source)
XLA Modules:
  0.0 114.7 jit_solution(5510369085726985654)
XLA Ops:
  0.0 106.7 %mlp_exchange.1 = (s32[1024,128]{1,0:T(8,128)}, bf16[512,2048]{1,0:T(8,128)(2,1)}, bf16[512,2048]{1,0:T(8,128)(2,1)}) custom-call(s32[1,1024]{1,0:T(1,128)} %bitcast.37, s32[4]{0:T(128)} %hot_ref.1, bf16[1024,2048]{1,0:T(8,128)(2,1)} %x_ref.1, bf16[2048,5632]{1,0:T(8,128)(2,1)} %wg_ref.1, bf16[2048,5632]{1,0:T(8,128)(2,1)} %wu_ref.1, ...), custom_call_target="tpu_custom_call" | custom-call | tf_op jit(solution)/shard_map/mlp_exchange/pallas_call | solution.py:339
  106.7 7.8 %unsort.1 = bf16[1024,2048]{1,0:T(8,128)(2,1)} custom-call(s32[1024,128]{1,0:T(8,128)} %get-tuple-element.8.place_ref, bf16[512,2048]{1,0:T(8,128)(2,1)} %get-tuple-element.9.back_ref, bf16[512,2048]{1,0:T(8,128)(2,1)} %get-tuple-element.10.kept_ref), custom_call_target="tpu_custom_call" | custom-call | tf_op jit(solution)/shard_map/unsort/pallas_call | solution.py:374
